TPU v7x, 256 devices: a whole 4x4x8 slice. The times are simulated.
256 devices in a mesh: dp: 32 (over z_lo, x, y), mp: 8 (over z_hi, core).
Axes of the slice: x: 4, y: 4, z: 8 (z_hi: 4, z_lo: 2; z = z_hi * 2 + z_lo), core: 2. Of those that a mesh axis runs over, the one named last changes fastest.
Arguments:
- hidden_states: bfloat16 [16384, 4096], P('dp', 'mp'), may hold values from -40 to 40
- norm_gain: float32 [1, 4096], replicated, may hold values from 0.1 to 1.9
- query_weight: bfloat16 [1, 4096, 4096], P(None, 'dp', 'mp'), may hold values from -0.01171875 to 0.01171875
- keyvalue_weight: bfloat16 [1, 4096, 2, 4096], P(None, 'dp', None, 'mp'), may hold values from -0.09375 to 0.09375
- output_weight: bfloat16 [1, 4096, 4096], P(None, 'dp', 'mp'), may hold values from -0.09375 to 0.09375
- position_bias: float32 [1, 32, 64], P(None, None, 'mp'), may hold values from -8 to 250
- lengths: int32 [128], P('dp'), may hold values from 16 to 128
Outputs:
- layer_output: bfloat16 [16384, 4096], P('dp', 'mp')
All inputs are finite; a program needn't handle non-finite values.
Results may differ from a plain program's by a relative error of at most 0.006.
Values may be sent and summed in bfloat16 or wider, within the bound.
A program may use at most 128 MiB of HBM per device.

v0:
```python
import jax
import jax.numpy as jnp
import numpy as np
from jax import lax
from jax.sharding import PartitionSpec as P

DH = 64
BUCKETS = 32
DIST = 128
LEN = 128


epsilon = 1e-06


def side_by_side(arrays, axis, dim, along):
    columns = [a.reshape(*a.shape[:along], -1) for a in arrays]
    both = jnp.concatenate(columns, axis=along)
    filled, at, outs = (lax.all_gather(both, axis, axis=dim, tiled=True), 0, [])
    for a, column in zip(arrays, columns):
        piece = filled[..., at : at + column.shape[along]]
        outs.append(piece.reshape(*piece.shape[:along], *a.shape[along:]))
        at += column.shape[along]
    return tuple(outs)


def bucket_table():
    half_count = BUCKETS // 2
    exact_count = half_count // 2
    positions = np.arange(LEN)
    relative = positions[None, :] - positions[:, None]
    distance = np.abs(relative)
    scaled = (
        np.log(np.maximum(distance, 1) / exact_count)
        / np.log(DIST / exact_count)
        * (half_count - exact_count)
    )
    far_bucket = np.minimum(exact_count + np.floor(scaled + 1e-09).astype(np.int32), half_count - 1)
    near_bucket = np.where(distance < exact_count, distance, far_bucket)
    return (near_bucket + np.where(relative > 0, half_count, 0)).astype(np.int32)


def normed_rows(hidden, gain_row):
    values = hidden.astype(jnp.float32)
    mean_square = jnp.mean(values * values, axis=-1, keepdims=True)
    return (values * lax.rsqrt(mean_square + epsilon) * gain_row).astype(jnp.bfloat16)


def add_projections(query_acc, pair_acc, normed, query_piece, pair_piece):
    query_acc = jnp.dot(normed, query_piece, preferred_element_type=jnp.float32)
    pair_acc = jnp.einsum("td,dcf->ctf", normed, pair_piece, preferred_element_type=jnp.float32)
    return (query_acc, pair_acc)


def local(
    hidden_states, norm_gain, query_weight, keyvalue_weight, output_weight, position_bias, lengths
):
    captions = lengths.shape[0]
    tokens_here = hidden_states.shape[0]
    heads_here = position_bias.shape[2]
    inner_here = heads_here * DH
    bucket_onehot = jnp.asarray(
        (bucket_table()[:, :, None] == np.arange(BUCKETS)[None, None, :]).astype(np.float32)
    )
    visible = jnp.arange(LEN)[None, :] < lengths[:, None]
    hidden = hidden_states
    gathered = lax.all_gather(hidden, "mp", axis=1, tiled=True)
    normed = normed_rows(gathered, norm_gain[0])
    zero_queries = jnp.zeros((tokens_here, inner_here), jnp.float32)
    zero_pairs = jnp.zeros((2, tokens_here, inner_here), jnp.float32)
    query_rows = query_weight[0]
    pair_rows = keyvalue_weight[0]
    out_rows = output_weight[0]
    shard_rows = side_by_side((query_rows, pair_rows, out_rows), "dp", 0, 1)
    query_acc, pair_acc = add_projections(
        zero_queries, zero_pairs, normed, shard_rows[0], shard_rows[1]
    )
    whole_rows = shard_rows[2]
    query_acc, pair_acc, out_full = (query_acc, pair_acc, whole_rows)
    queries = query_acc.astype(jnp.bfloat16).reshape(captions, LEN, heads_here, DH)
    key_rows = pair_acc[0].astype(jnp.bfloat16).reshape(captions, LEN, heads_here, DH)
    value_rows = pair_acc[1].astype(jnp.bfloat16).reshape(captions, LEN, heads_here, DH)
    position_terms = jnp.einsum(
        "qkb,bh->hqk", bucket_onehot, position_bias[0], precision=lax.Precision.HIGHEST
    )
    scores = (
        jnp.einsum("cqhe,ckhe->chqk", queries, key_rows, preferred_element_type=jnp.float32)
        + position_terms[None]
    )
    scores = jnp.where(visible[:, None, None, :], scores, -1e30)
    maxima = jnp.max(scores, axis=-1, keepdims=True)
    raised = jnp.exp(scores - maxima)
    weights = (raised / jnp.sum(raised, axis=-1, keepdims=True)).astype(jnp.bfloat16)
    mixture = jnp.einsum("chqk,ckhe->cqhe", weights, value_rows, preferred_element_type=jnp.float32)
    attended = mixture.astype(jnp.bfloat16).reshape(tokens_here, inner_here)
    partial_out = jnp.einsum("tf,df->td", attended, out_full, preferred_element_type=jnp.float32)
    reduced = lax.psum_scatter(
        partial_out.astype(jnp.bfloat16), "mp", scatter_dimension=1, tiled=True
    ).astype(jnp.float32)
    hidden = (hidden.astype(jnp.float32) + reduced).astype(jnp.bfloat16)
    return hidden


def solution(mesh):
    in_specs = (
        P("dp", "mp"),
        P(),
        P(None, "dp", "mp"),
        P(None, "dp", None, "mp"),
        P(None, "dp", "mp"),
        P(None, None, "mp"),
        P("dp"),
    )
    out_specs = P("dp", "mp")
    return jax.shard_map(local, mesh=mesh, in_specs=in_specs, out_specs=out_specs, check_vma=False)
```

profile of v0, /device:TPU:1, one launch (start us, length us, event | category | flops | bytes accessed | tf_op | source)
XLA Modules:
  0.0 411.3 jit_solution(2870992319001672972)
XLA Ops:
  6.5 0.0 copy-start
  6.5 0.7 all-gather.5.cloned.1.call-update
  7.3 0.0 all-gather.3.cloned.1.call-start
  7.3 1.2 copy.28
  8.5 1.0 copy.17
  9.5 1.0 copy.19
  10.5 0.8 pad_maximum_fusion
  11.4 0.0 all-gather.3.cloned.1.call-update
  11.4 0.0 reduce-scatter.2.cloned.1.call-start
  11.4 1.2 convolution_bitcast_fusion
  12.7 0.2 copy.23
  12.9 0.0 copy-done.5
  12.9 0.1 iota_compare_fusion
  13.0 53.4 %all-gather.5.cloned.1.call-done = bf16[512,4096]{1,0:T(8,128)(2,1)} async-done(((bf16[512,512]{1,0:T(8,128)(2,1)}), bf16[512,4096]{1,0:T(8,128)(2,1)}) %all-gather.5.cloned.1.call-update) | async-done | bytes 4194320 | tf_op jit(solution)/shard_map/all_gather | solution.py:67
  66.4 3.1 fusion.1
  69.5 0.0 copy-start.4
  69.5 222.5 %all-gather.3.cloned.1.call-done = bf16[4096,2048]{0,1:T(8,128)(2,1)} async-done(((bf16[128,2048]{0,1:T(8,128)(2,1)}), bf16[4096,2048]{0,1:T(8,128)(2,1)}) %all-gather.3.cloned.1.call-update) | async-done | bytes 16777232 | tf_op jit(solution)/shard_map/all_gather | solution.py:19
  292.0 7.9 %slice.22 = bf16[4096,1024]{0,1:T(8,128)(2,1)} slice(bf16[4096,2048]{0,1:T(8,128)(2,1)} %all-gather.3.cloned.1.call-done), slice={[0:4096], [512:1536]} | slice | bytes 16777216 | tf_op jit(solution)/shard_map/slice | solution.py:21
  299.9 7.3 %fusion.13 = bf16[2,512,512]{1,2,0:T(8,128)(2,1)S(1)} fusion(bf16[4096,2,512]{0,2,1:T(8,128)(2,1)} %bitcast.35, bf16[512,4096]{1,0:T(8,128)(2,1)S(1)} %copy-done.1, f32[4096]{0:T(1024)S(1)} %bitcast.40, f32[512]{0:T(512)S(1)} %add_rsqrt_fusion), kind=kOutput, calls=%fused_computation.17 | convolution fusion | flops 4303880192 | bytes 13649920 | tf_op jit(solution)/shard_map/td,dcf->ctf/dot_general | solution.py:51
  307.2 0.1 fusion.45
  307.3 0.1 convert_element_type.45
  307.4 5.8 %fusion.16 = bf16[512,512]{1,0:T(8,128)(2,1)S(1)} fusion(bf16[4096,2048]{0,1:T(8,128)(2,1)} %all-gather.3.cloned.1.call-done, bf16[512,4096]{1,0:T(8,128)(2,1)} %all-gather.5.cloned.1.call-done, f32[4096]{0:T(1024)S(1)} %bitcast.41, f32[512]{0:T(512)S(1)} %add_rsqrt_fusion), kind=kOutput, calls=%fused_computation.18 | convolution fusion | flops 2156134400 | bytes 8931328 | tf_op jit(solution)/shard_map/dot_general | solution.py:50
  313.3 0.5 reshape.48
  313.8 0.1 convert_element_type.43
  314.0 2.5 fusion.46
  316.5 2.0 fusion.19
  318.5 0.4 copy.26
  318.9 6.5 %convolution_convert_fusion = bf16[512,4096]{1,0:T(8,128)(2,1)} fusion(bf16[4096,2048]{0,1:T(8,128)(2,1)} %all-gather.3.cloned.1.call-done, bf16[64,8,4,128]{3,2,1,0:T(4,128)(2,1)S(1)} %bitcast.36), kind=kOutput, calls=%fused_computation.6 | convolution fusion | flops 2149580800 | bytes 8912896 | tf_op jit(solution)/shard_map/tf,df->td/dot_general | solution.py:96
  325.4 0.0 reduce-scatter.2.cloned.1.call-update
  325.5 77.3 %reduce-scatter.2.cloned.1.call-done = bf16[512,512]{1,0:T(8,128)(2,1)} async-done(((bf16[512,4096]{1,0:T(8,128)(2,1)}), bf16[512,512]{1,0:T(8,128)(2,1)}) %reduce-scatter.2.cloned.1.call-update) | async-done | bytes 524304 | tf_op jit(solution)/shard_map/reduce_scatter | solution.py:97
  402.8 0.0 copy-done.3
  402.8 2.0 add_convert_fusion
  (10 shorter events, 0.0 us)
Async XLA Ops:
  6.5 4.9 %copy-start = (f32[1,32,8]{1,2,0:T(8,128)S(1)}, f32[1,32,8]{1,2,0:T(8,128)}, u32[]{:S(2)}) copy-start(f32[1,32,8]{1,2,0:T(8,128)} %param.13) | copy-start | bytes 3076
  6.5 4.9 %copy-start.2 = (f32[128,128,32]{1,2,0:T(8,128)S(1)}, f32[128,128,32]{1,2,0:T(8,128)}, u32[]{:S(2)}) copy-start(f32[128,128,32]{1,2,0:T(8,128)} %constant.13.clone) | copy-start | bytes 6291460
  6.5 6.4 %copy-start.5 = (s32[4]{0:T(128)S(1)}, s32[4]{0:T(128)}, u32[]{:S(2)}) copy-start(s32[4]{0:T(128)} %param.14) | copy-start | bytes 52
  6.5 59.8 %all-gather.5.cloned.1.call-start = ((), (), s32[]{:S(2)}) async-start(), calls=%async_computation.2 | async-start | bytes 4718592 | tf_op jit(solution)/shard_map/all_gather | solution.py:67
  7.3 284.8 %all-gather.3.cloned.1.call-start = ((), (), s32[]{:S(2)}) async-start(), calls=%async_computation.1 | async-start | bytes 17301504 | tf_op jit(solution)/shard_map/all_gather | solution.py:19
  11.4 391.4 %reduce-scatter.2.cloned.1.call-start = ((), (), s32[]{:S(2)}) async-start(), calls=%async_computation.3 | async-start | bytes 4718592 | tf_op jit(solution)/shard_map/reduce_scatter | solution.py:97
  69.5 230.4 %copy-start.4 = (f32[1,4096]{1,0:T(1,128)S(1)}, f32[1,4096]{1,0:T(1,128)}, u32[]{:S(2)}) copy-start(f32[1,4096]{1,0:T(1,128)} %param.9) | copy-start | bytes 49156
  292.0 7.9 %copy-start.1 = (bf16[512,4096]{1,0:T(8,128)(2,1)S(1)}, bf16[512,4096]{1,0:T(8,128)(2,1)}, u32[]{:S(2)}) copy-start(bf16[512,4096]{1,0:T(8,128)(2,1)} %all-gather.5.cloned.1.call-done) | copy-start | bytes 12582916
  325.4 77.4 %copy-start.3 = (bf16[512,512]{1,0:T(8,128)(2,1)S(1)}, bf16[512,512]{1,0:T(8,128)(2,1)}, u32[]{:S(2)}) copy-start(bf16[512,512]{1,0:T(8,128)(2,1)} %param.8) | copy-start | bytes 1572868
Sparse Core Ops, SparseCore 0:
  9.2 57.1 all-gather.4
  68.1 223.8 all-gather.2
  325.6 77.1 reduce-scatter.1
where the time goes:
time: 413 us; the launch traced here: 411 us
  waiting for transfers between devices  354 us (86%)
  matrix products  25.4 us (6%)
  between operations  13.2 us (3%)
  local copies, waits for them, and re-layouts  12.6 us (3%)
  other arithmetic  6 us (1%)
    all_gather x1, waiting for transfers between devices, side_by_side(): filled, at, outs = (lax.all_gather(both, axis, axis=dim, tiled=True), 0, [])  223 us
    reduce_scatter x1, waiting for transfers between devices, local(): lax.psum_scatter(partial_out.astype(jnp.bfloat16), 'mp', scatter_dimensio...  77.3 us
    all_gather x1, waiting for transfers between devices, local(): gathered = lax.all_gather(hidden, 'mp', axis=1, tiled=True)  53.4 us
  transfers between devices with their start and end apart: 3, of which 3 were waited for; matrix products, arithmetic and copies ran while one was open for 2% of the time, Pallas kernels for 0%

commit v1 on v0

v1 whole, which is shorter than its diff:
```python
import functools

import jax
import jax.numpy as jnp
import numpy as np
from jax import lax
from jax.experimental import pallas as pl
from jax.experimental.pallas import tpu as pltpu
from jax.sharding import PartitionSpec as P

MESH = pl.DeviceIdType.MESH
DH = 64
BUCKETS = 32
DIST = 128
LEN = 128
EPS = 1e-06
F32 = jnp.float32
BF16 = jnp.bfloat16
NT = (((1,), (1,)), ((), ()))


def far_steps():
    half = BUCKETS // 2
    exact = half // 2
    distance = np.arange(LEN)
    scaled = np.log(np.maximum(distance, 1) / exact) / np.log(DIST / exact) * (half - exact)
    far = np.minimum(exact + np.floor(scaled + 1e-09).astype(np.int32), half - 1)
    near = np.where(distance < exact, distance, far)
    return [int(np.min(distance[near >= b])) for b in range(1, half) if np.any(near >= b)]


STEPS = far_steps()


def kernel(x_ref, g_ref, w_ref, pb_ref, mk_ref, o_ref,
           wb, hb, nb, qkv, att, ob, sb, rb, bt, pbs, mks, fs, fr,
           loc_sem, send_sem, hr, hd, wzs, wf, ws, wd, rr, sm, fin):
    dp = lax.axis_index("dp")
    mp = lax.axis_index("mp")
    zl, xi, yi = dp // 16, (dp // 4) % 4, dp % 4
    zh, c = mp // 2, mp % 2
    z = zh * 2 + zl
    oc = 1 - c
    oz = 1 - zl

    def dev(zz, xx, yy, cc):
        return ((zz % 2) * 16 + xx * 4 + yy, (zz // 2) * 2 + cc)

    xr, xl = (xi + 1) % 4, (xi + 3) % 4
    yr, yl = (yi + 1) % 4, (yi + 3) % 4
    zr, zf = (z + 1) % 8, (z + 7) % 8
    d_xr, d_xl = dev(z, xr, yi, c), dev(z, xl, yi, c)
    d_yr, d_yl = dev(z, xi, yr, c), dev(z, xi, yl, c)
    d_zr, d_zl = dev(zr, xi, yi, c), dev(zf, xi, yi, c)
    d_pc = dev(z, xi, yi, oc)
    d_zp = dev(zh * 2 + oz, xi, yi, c)

    pending = []

    def send(src, dst, sem, to, group):
        d = pltpu.make_async_remote_copy(
            src_ref=src, dst_ref=dst, send_sem=send_sem.at[group], recv_sem=sem,
            device_id=to, device_id_type=MESH)
        d.start()
        pending.append(d)

    def recv(dst, sem):
        pltpu.make_async_remote_copy(
            src_ref=dst, dst_ref=dst, send_sem=send_sem.at[0], recv_sem=sem,
            device_id=d_pc, device_id_type=MESH).wait_recv()

    barrier = pltpu.get_barrier_semaphore()
    for to in (d_xr, d_xl, d_yr, d_yl, d_zr, d_zl, d_pc):
        pl.semaphore_signal(barrier, inc=1, device_id=to, device_id_type=MESH)
    pl.semaphore_wait(barrier, 7)

    def blk(k, cls, f, s, h=None):
        zz = zl if cls == 0 else oz
        bx, by = (f, s) if cls == 0 else (s, f)
        if h is None:
            return wb.at[pl.ds(2 * k, 2), c, zz, bx, by]
        return wb.at[2 * k + h, c, zz, bx, by]

    def axes(cls):
        if cls == 0:
            return xi, xr, xl, d_xr, d_xl, yi, yr, yl, d_yr, d_yl
        return yi, yr, yl, d_yr, d_yl, xi, xr, xl, d_xr, d_xl

    def fo(cls, o):
        f = axes(cls)[0]
        return (f + (0, 3, 1, 2)[o]) % 4

    def S0(cls, k, src):
        f, fR, fL, dfR, dfL, s, sR, sL, dsR, dsL = axes(cls)
        own = blk(k, cls, f, s)
        send(src, own, wf.at[cls, k, 0], dfR, 0)
        send(src, own, wf.at[cls, k, 1], dfL, 0)
        send(src, own, ws.at[cls, k, 0, 0], dsR, 0)
        send(src, own, ws.at[cls, k, 0, 1], dsL, 0)

    def S1(cls, k):
        f, fR, fL, dfR, dfL, s, sR, sL, dsR, dsL = axes(cls)
        recv(blk(k, cls, fL, s), wf.at[cls, k, 0])
        recv(blk(k, cls, fR, s), wf.at[cls, k, 1])
        send(blk(k, cls, fL, s, 0), blk(k, cls, fL, s, 0), wf.at[cls, k, 2], dfR, 0)
        send(blk(k, cls, fR, s, 1), blk(k, cls, fR, s, 1), wf.at[cls, k, 3], dfL, 0)
        for o, ff in ((1, fL), (2, fR)):
            b = blk(k, cls, ff, s)
            send(b, b, ws.at[cls, k, o, 0], dsR, 0)
            send(b, b, ws.at[cls, k, o, 1], dsL, 0)

    def S2(cls, k):
        f, fR, fL, dfR, dfL, s, sR, sL, dsR, dsL = axes(cls)
        ff = (f + 2) % 4
        recv(blk(k, cls, ff, s, 0), wf.at[cls, k, 2])
        recv(blk(k, cls, ff, s, 1), wf.at[cls, k, 3])
        b = blk(k, cls, ff, s)
        send(b, b, ws.at[cls, k, 3, 0], dsR, 0)
        send(b, b, ws.at[cls, k, 3, 1], dsL, 0)

    def Y(cls, k, o):
        f, fR, fL, dfR, dfL, s, sR, sL, dsR, dsL = axes(cls)
        ff = fo(cls, o)
        recv(blk(k, cls, ff, sL), ws.at[cls, k, o, 0])
        recv(blk(k, cls, ff, sR), ws.at[cls, k, o, 1])
        send(blk(k, cls, ff, sL, 0), blk(k, cls, ff, sL, 0), ws.at[cls, k, o, 2], dsR, 0)
        send(blk(k, cls, ff, sR, 1), blk(k, cls, ff, sR, 1), ws.at[cls, k, o, 3], dsL, 0)

    def dslice(k, cls, ff, cc):
        if cls == 0:
            return wb.at[pl.ds(2 * k, 2), cc, zl, ff]
        return wb.at[pl.ds(2 * k, 2), cc, oz, :, ff]

    def Z(cls, k, o):
        f, fR, fL, dfR, dfL, s, sR, sL, dsR, dsL = axes(cls)
        ff = fo(cls, o)
        s2 = (s + 2) % 4
        recv(blk(k, cls, ff, s2, 0), ws.at[cls, k, o, 2])
        recv(blk(k, cls, ff, s2, 1), ws.at[cls, k, o, 3])
        piece = dslice(k, cls, ff, c)
        send(piece, piece, wd.at[cls, k, o], d_pc, 0)

    def hpiece(zo, hh, j):
        return hb.at[(zo // 2) * 2 + hh, pl.ds(((zo % 2) * 2 + j) * LEN, LEN)]

    def hsend(right, r, hh):
        zo = (z - r + 8) % 8 if right else (z + r) % 8
        for j in range(2):
            p = hpiece(zo, hh, j)
            send(p, p, hr.at[0 if right else 1, r, hh, j], d_zr if right else d_zl, 0)

    def hrecv(right, r, hh):
        zo = (z - 1 - r + 8) % 8 if right else (z + 1 + r) % 8
        for j in range(2):
            recv(hpiece(zo, hh, j), hr.at[0 if right else 1, r, hh, j])

    def hstep(r, hh):
        for right in (True, False):
            full = r < 3 or (hh == 0) == right
            if not full:
                continue
            hrecv(right, r, hh)
            if r + 1 < 3 or (r + 1 == 3 and (hh == 0) == right):
                hsend(right, r + 1, hh)

    w_own = [w_ref.at[zl, pl.ds(2 * k, 2)] for k in range(2)]
    w_far = [w_ref.at[oz, pl.ds(2 * k, 2)] for k in range(2)]
    for j in range(2):
        send(x_ref.at[pl.ds((oc * 2 + j) * LEN, LEN)],
             hb.at[mp, pl.ds((zl * 2 + j) * LEN, LEN)], hd.at[j], d_pc, 0)
    for k in range(2):
        send(w_far[k], wb.at[pl.ds(2 * k, 2), c, zl, xi, yi], wzs.at[k], d_zp, 0)
    for k in range(2):
        S0(0, k, w_own[k])
    send(pb_ref.at[pl.ds(zl * 4, 4)], pbs.at[c], sm.at[0], d_pc, 0)
    send(mk_ref, mks.at[zl], sm.at[1], d_zp, 0)
    locs = []
    for j in range(2):
        locs.append(pltpu.make_async_copy(
            x_ref.at[pl.ds((c * 2 + j) * LEN, LEN)],
            hb.at[mp, pl.ds((zl * 2 + j) * LEN, LEN)], loc_sem.at[j]))
    for k in range(2):
        locs.append(pltpu.make_async_copy(w_own[k], blk(k, 0, xi, yi), loc_sem.at[2 + k]))
    locs.append(pltpu.make_async_copy(pb_ref.at[pl.ds(zl * 4, 4)], pbs.at[c], loc_sem.at[4]))
    locs.append(pltpu.make_async_copy(mk_ref, mks.at[zl], loc_sem.at[5]))
    for d in locs:
        d.start()
    for d in locs:
        d.wait()
    for j in range(2):
        recv(hb.at[zh * 2 + oc, pl.ds((zl * 2 + j) * LEN, LEN)], hd.at[j])
    for hh in range(2):
        hsend(True, 0, hh)
        hsend(False, 0, 1 - hh)

    def zx(k):
        b = blk(k, 1, yi, xi)
        recv(b, wzs.at[k])
        S0(1, k, b)

    S1(0, 0)
    zx(0)
    S1(0, 1)
    zx(1)
    hstep(0, 0)
    Y(0, 0, 0)
    Y(0, 1, 0)
    hstep(0, 1)
    S1(1, 0)
    Y(1, 0, 0)
    S1(1, 1)
    Y(1, 1, 0)
    S2(0, 0)
    S2(0, 1)
    hstep(1, 0)
    S2(1, 0)
    S2(1, 1)
    for cls in range(2):
        Y(cls, 0, 1)
        Y(cls, 0, 2)
    hstep(1, 1)
    for cls in range(2):
        Y(cls, 1, 1)
        Y(cls, 1, 2)
        Z(cls, 0, 0)
        Z(cls, 1, 0)

    recv(pbs.at[oc], sm.at[0])
    recv(mks.at[oz], sm.at[1])
    row = lax.broadcasted_iota(jnp.int32, (LEN, LEN), 0)
    col = lax.broadcasted_iota(jnp.int32, (LEN, LEN), 1)
    rel = col - row
    dist = jnp.abs(rel)
    bucket = jnp.where(rel > 0, BUCKETS // 2, 0)
    for t in STEPS:
        bucket = bucket + jnp.where(dist >= t, 1, 0)

    def bias_head(i, _):
        cc, h = i // 4, i % 4
        tab = jnp.zeros((LEN, LEN), F32)
        for b in range(BUCKETS):
            tab = jnp.where(bucket == b, pbs[cc, h, pl.ds(b, 1), :], tab)
        bt[cc, pl.ds(pl.multiple_of(h * LEN, LEN), LEN), :] = tab
        return 0

    lax.fori_loop(0, 8, bias_head, 0)

    hstep(2, 0)
    for cls in range(2):
        Y(cls, 0, 3)
    for cls in range(2):
        Y(cls, 1, 3)
    hstep(2, 1)
    for o in (1, 2):
        for cls in range(2):
            Z(cls, 0, o)
            Z(cls, 1, o)
    hstep(3, 0)
    hstep(3, 1)
    for cls in range(2):
        Z(cls, 0, 3)
        Z(cls, 1, 3)

    def norm_rows(i, _):
        rows = pl.ds(pl.multiple_of(i * 16, 16), 16)
        total = jnp.zeros((16, 512), F32)
        for fb in range(8):
            v = hb[fb, rows, :].astype(F32)
            total = total + v * v
        ms = jnp.sum(total, axis=-1, keepdims=True) * (1.0 / 4096.0)
        scale = lax.rsqrt(ms + EPS)
        for fb in range(8):
            v = hb[fb, rows, :].astype(F32)
            nb[rows, fb * 512:(fb + 1) * 512] = (
                v * scale * g_ref[:, fb * 512:(fb + 1) * 512]).astype(BF16)
        return 0

    lax.fori_loop(0, 32, norm_rows, 0)

    for o in range(4):
        for cls in range(2):
            for k in range(2):
                ff = fo(cls, o)
                recv(dslice(k, cls, ff, oc), wd.at[cls, k, o])

    def project(i, _):
        m, cc = i // 2, i % 2
        w = wb[m, cc].reshape(4096, 256)
        qkv[m, cc] = jnp.dot(nb[...], w, preferred_element_type=F32).astype(BF16)
        return 0

    lax.fori_loop(0, 6, project, 0)

    head = lax.broadcasted_iota(jnp.int32, (LEN, 256), 1) // DH

    def attend(i, _):
        cap, cc = i // 2, i % 2
        rows = pl.ds(pl.multiple_of(cap * LEN, LEN), LEN)
        q, kk, v = qkv[0, cc, rows, :], qkv[1, cc, rows, :], qkv[2, cc, rows, :]
        zero = jnp.zeros((), BF16)
        qm = jnp.concatenate([jnp.where(head == h, q, zero) for h in range(4)], axis=0)
        s = lax.dot_general(qm, kk, NT, preferred_element_type=F32) + bt[cc]
        seen = mks[cap // 2, pl.ds(2 * c + cap % 2, 1), :]
        s = jnp.where(seen > 0.5, s, -1e30)
        top = jnp.max(s, axis=-1, keepdims=True)
        e = jnp.exp(s - top)
        w = (e / jnp.sum(e, axis=-1, keepdims=True)).astype(BF16)
        mix = jnp.dot(w, v, preferred_element_type=F32)
        out = jnp.zeros((LEN, 256), F32)
        for h in range(4):
            out = jnp.where(head == h, mix[h * LEN:(h + 1) * LEN], out)
        att[cc, rows, :] = out.astype(BF16)
        return 0

    lax.fori_loop(0, 8, attend, 0)

    def out_block(zq):
        for hh in range(2):
            total = None
            for cc in range(2):
                w = wb[3, cc, hh_zl(zq, hh), hh_x(zq, hh)].reshape(512, 256)
                part = lax.dot_general(att[cc], w, NT, preferred_element_type=F32)
                total = part if total is None else total + part
            ob[zq * 2 + hh] = total

    def hh_zl(zq, hh):
        return (zq * 2 + hh) // 4

    def hh_x(zq, hh):
        return (zq * 2 + hh) % 4

    def own(dz, hh, j):
        return ob[(dz // 2) * 2 + hh, pl.ds(((dz % 2) * 2 + j) * LEN, LEN), :]

    def rs_round(r):
        for j in range(2):
            for hh in range(2):
                for right in (True, False):
                    side = 0 if right else 1
                    first = (hh == 0) == right
                    dz = (z + 4 - r) % 8 if right else (z + 4 + r) % 8
                    if r == 0 and not first:
                        continue
                    value = own(dz, hh, j)
                    if r >= 2 or (r == 1 and first):
                        recv(rb.at[side, r - 1, hh, j], rr.at[side, r - 1, hh, j])
                        value = value + rb[side, r - 1, hh, j].astype(F32)
                    sb[side, r, hh, j] = value.astype(BF16)
                    send(sb.at[side, r, hh, j], rb.at[side, r, hh, j],
                         rr.at[side, r, hh, j], d_zr if right else d_zl, 0)

    out_block((zh + 2) % 4)
    rs_round(0)
    out_block((zh + 1) % 4)
    out_block((zh + 3) % 4)
    rs_round(1)
    out_block(zh)
    rs_round(2)
    rs_round(3)

    def finish(hh, j):
        for side in range(2):
            recv(rb.at[side, 3, hh, j], rr.at[side, 3, hh, j])
        rows = pl.ds((zl * 2 + j) * LEN, LEN)
        return (hb[zh * 2 + hh, rows, :].astype(F32) + own(z, hh, j)
                + rb[0, 3, hh, j].astype(F32) + rb[1, 3, hh, j].astype(F32)).astype(BF16)

    for j in range(2):
        fs[j] = finish(oc, j)
        send(fs.at[j], fr.at[j], fin.at[j], d_pc, 0)
        o_ref[pl.ds((c * 2 + j) * LEN, LEN), :] = finish(c, j)
    for j in range(2):
        recv(fr.at[j], fin.at[j])
        o_ref[pl.ds((oc * 2 + j) * LEN, LEN), :] = fr[j]

    for d in pending:
        d.wait_send()


def local(hidden_states, norm_gain, query_weight, keyvalue_weight, output_weight,
          position_bias, lengths):
    kv = jnp.transpose(keyvalue_weight[0], (1, 0, 2))
    w = jnp.stack([query_weight[0], kv[0], kv[1], output_weight[0]])
    w = jnp.transpose(w.reshape(4, 128, 2, 256), (2, 0, 1, 3))
    pb = jnp.broadcast_to(jnp.transpose(position_bias[0])[:, :, None], (8, BUCKETS, LEN))
    mask = (jnp.arange(LEN)[None, :] < lengths[:, None]).astype(F32)
    mask = jnp.concatenate([mask, jnp.zeros((4, LEN), F32)])
    vm = pl.BlockSpec(memory_space=pltpu.VMEM)
    dma = pltpu.SemaphoreType.DMA
    return pl.pallas_call(
        kernel,
        out_shape=jax.ShapeDtypeStruct((512, 512), BF16),
        in_specs=[vm] * 5,
        out_specs=vm,
        scratch_shapes=[
            pltpu.VMEM((4, 2, 2, 4, 4, 128, 256), BF16),
            pltpu.VMEM((8, 512, 512), BF16),
            pltpu.VMEM((512, 4096), BF16),
            pltpu.VMEM((3, 2, 512, 256), BF16),
            pltpu.VMEM((2, 512, 256), BF16),
            pltpu.VMEM((8, 512, 512), F32),
            pltpu.VMEM((2, 4, 2, 2, 128, 512), BF16),
            pltpu.VMEM((2, 4, 2, 2, 128, 512), BF16),
            pltpu.VMEM((2, 512, 128), F32),
            pltpu.VMEM((2, 4, BUCKETS, LEN), F32),
            pltpu.VMEM((2, 8, LEN), F32),
            pltpu.VMEM((2, 128, 512), BF16),
            pltpu.VMEM((2, 128, 512), BF16),
            dma((6,)),
            dma((1,)),
            dma((2, 4, 2, 2)),
            dma((2,)),
            dma((2,)),
            dma((2, 2, 4)),
            dma((2, 2, 4, 4)),
            dma((2, 2, 4)),
            dma((2, 4, 2, 2)),
            dma((2,)),
            dma((2,)),
        ],
        compiler_params=pltpu.CompilerParams(
            collective_id=0, has_side_effects=True, vmem_limit_bytes=60 * 1024 * 1024),
        name="t5_attention",
    )(hidden_states, norm_gain, w, pb, mask)


def solution(mesh):
    in_specs = (
        P("dp", "mp"),
        P(),
        P(None, "dp", "mp"),
        P(None, "dp", None, "mp"),
        P(None, "dp", "mp"),
        P(None, None, "mp"),
        P("dp"),
    )
    return jax.shard_map(local, mesh=mesh, in_specs=in_specs, out_specs=P("dp", "mp"), check_vma=False)
```

time: 413 us -> 128 us (0.31)
  waiting for transfers between devices: 354 us -> 0 us
  Pallas kernels: 0 us -> 121 us
  matrix products: 25.4 us -> 0 us
  between operations: 13.2 us -> 0.06 us
  local copies, waits for them, and re-layouts: 12.6 us -> 5.75 us
  other arithmetic: 6 us -> 0.73 us
    all_gather x2 -> x0, waiting for transfers between devices: 276 us -> none  [the longest x1 223 us: side_by_side(): filled, at, outs = (lax.all_gather(both, axis, axis=dim, tiled=True), 0, [])]
    pallas_call x0 -> x1, Pallas kernels: none -> 121 us  [local(): pl.pallas_call(kernel, out_shape=jax.ShapeDtypeStruct((512, 512), BF16),...]
    reduce_scatter x1 -> x0, waiting for transfers between devices: 77.3 us -> none  [local(): lax.psum_scatter(partial_out.astype(jnp.bfloat16), 'mp', scatter_dimensio...]
    dot_general x5 -> x0, matrix products: 22.9 us -> none  [the longest x1 7.31 us: add_projections(): jnp.einsum('td,dcf->ctf', normed, pair_piece, preferred_element_type=jnp....]
    slice x2 -> x0, local copies, waits for them, and re-layouts: 7.94 us -> none  [the longest x1 7.87 us: side_by_side(): piece = filled[..., at:at + column.shape[along]]]
  transfers between devices with their start and end apart: 3 -> 0, of which waited for: 3 -> 0; matrix products, arithmetic and copies ran while one was open for 2% -> 0% of each run, Pallas kernels for 0% -> 0%
where the time goes in v1:
time: 128 us
  Pallas kernels  121 us (95%)
  local copies, waits for them, and re-layouts  5.75 us (4%)
    pallas_call x1, Pallas kernels, local(): pl.pallas_call(kernel, out_shape=jax.ShapeDtypeStruct((512, 512), BF16),...  121 us
    unnamed x12, local copies, waits for them, and re-layouts  4 us

profile of v1, /device:TPU:1, one launch (start us, length us, event | category | flops | bytes accessed | tf_op | source)
XLA Modules:
  0.0 128.0 jit_solution(6837111995157647129)
XLA Ops:
  0.0 0.0 copy-start.3
  0.0 0.7 copy-done.3
  0.7 0.1 iota_compare_fusion
  0.7 0.6 pad_convert_fusion.mk_ref
  1.3 0.0 copy-start.1
  1.3 0.0 copy-start.2
  1.3 1.1 copy.11
  2.4 0.0 copy-done.1
  2.4 0.0 copy-start
  2.4 0.1 copy.12
  2.5 0.0 copy-done.2
  2.5 0.7 broadcast_in_dim.2.pb_ref
  3.3 0.1 copy-done
  3.4 0.2 copy.10
  3.6 0.1 pad_maximum_fusion
  3.7 1.0 copy.13
  4.7 121.5 %t5_attention.1 = bf16[512,512]{1,0:T(8,128)(2,1)} custom-call(bf16[512,512]{1,0:T(8,128)(2,1)} %x_ref.1, f32[1,4096]{1,0:T(1,128)} %g_ref.1, bf16[2,4,128,256]{3,2,1,0:T(8,128)(2,1)} %bitcast.9, f32[8,32,128]{2,1,0:T(8,128)} %broadcast_in_dim.2.pb_ref, f32[8,128]{1,0:T(8,128)} %pad_convert_fusion.mk_ref), custom_call_target="tpu_custom_call" | custom-call | tf_op jit(solution)/shard_map/t5_attention/pallas_call | solution.py:390
  126.2 1.9 %copy.15 = bf16[512,512]{1,0:T(8,128)(2,1)} copy(bf16[512,512]{1,0:T(8,128)(2,1)} %t5_attention.1) | data formatting | bytes 1048576
Async XLA Ops:
  0.0 0.7 copy-start.3
  1.3 1.1 copy-start.1
  1.3 1.2 copy-start.2
  2.4 1.0 copy-start

commit v2 on v0

v2 whole, which is shorter than its diff:
```python
import functools

import jax
import jax.numpy as jnp
import numpy as np
from jax import lax
from jax.experimental import pallas as pl
from jax.experimental.pallas import tpu as pltpu
from jax.sharding import PartitionSpec as P

MESH = pl.DeviceIdType.MESH
DH = 64
BUCKETS = 32
DIST = 128
LEN = 128
EPS = 1e-06
F32 = jnp.float32
BF16 = jnp.bfloat16
NT = (((1,), (1,)), ((), ()))


def far_steps():
    half = BUCKETS // 2
    exact = half // 2
    distance = np.arange(LEN)
    scaled = np.log(np.maximum(distance, 1) / exact) / np.log(DIST / exact) * (half - exact)
    far = np.minimum(exact + np.floor(scaled + 1e-09).astype(np.int32), half - 1)
    near = np.where(distance < exact, distance, far)
    return [int(np.min(distance[near >= b])) for b in range(1, half) if np.any(near >= b)]


STEPS = far_steps()


LINKS = ("x+", "x-", "y+", "y-", "z+", "z-", "d")
RATE = {"d": 400e3}
COST = {"norm": 1.0, "proj": 0.9, "attn": 0.55, "out": 0.5, "bias": 2.2, "rs": 0.25, "fin": 0.4}
AHEAD = 3.0


def flip(d):
    return "-" if d == "+" else "+"


def make_tasks():
    tasks = {}

    def add(tid, link, kib, needs, rank):
        tasks[tid] = (link, kib, tuple(needs), rank)

    for j in range(2):
        add(("HD", j), "d", 128, (), 0)
    for m in range(4):
        add(("ZX", m), "z", 64, (), 0.5 if m < 3 else 14)
    for j in range(2):
        for d in "+-":
            for r in range(4):
                for hh in range(2):
                    if r == 3 and (hh == 0) != (d == "+"):
                        continue
                    need = [("HD", j)] if r == 0 and hh == 1 else []
                    if r > 0:
                        need = [("H", d, r - 1, hh, j)]
                    add(("H", d, r, hh, j), "z" + d, 128, need, 1 + 20 * j + r)
    for m in range(4):
        late = 10 if m == 3 else 0
        for cls in range(2):
            fa, sa = ("x", "y") if cls == 0 else ("y", "x")
            base = [("ZX", m)] if cls else []
            for d in "+-":
                add(("F", cls, m, d), fa + d, 64, base, m + late)
                add(("S", cls, m, 0, d), sa + d, 64, base, m + late + 1)
                add(("S", cls, m, 1, d), sa + d, 64, [("F", cls, m, "+")], m + late + 1)
                add(("S", cls, m, 2, d), sa + d, 64, [("F", cls, m, "-")], m + late + 1)
                add(("S", cls, m, 3, d), sa + d, 64, [("F2", cls, m)], m + late)
            d = "+-"[(m + cls) % 2]
            add(("F2", cls, m), fa + d, 64, [("F", cls, m, d)], m + late - 1)
            for o in range(4):
                d = "+-"[(m + cls + o) % 2]
                add(("S2", cls, m, o), sa + d, 64, [("S", cls, m, o, d)], m + late + 0.5)
                add(("D", cls, m, o), "d", 256,
                    [("S", cls, m, o, "+"), ("S", cls, m, o, "-"), ("S2", cls, m, o)], m + late)

    def mine(m):
        return ([("ZX", m)] + [("F", c, m, d) for c in range(2) for d in "+-"]
                + [("F2", c, m) for c in range(2)]
                + [("S", c, m, o, d) for c in range(2) for o in range(4) for d in "+-"]
                + [("S2", c, m, o) for c in range(2) for o in range(4)])

    def theirs(m):
        return [("D", c, m, o) for c in range(2) for o in range(4)]

    add(("bias",), None, 0, (), 60)
    for j in range(2):
        add(("norm", j), None, 0,
            [("HD", j)] + [t for t in tasks if t[0] == "H" and t[4] == j], 40 + j)
        for m in range(3):
            add(("proj", m, 0, j), None, 0, [("norm", j)] + mine(m), 42 + 20 * j + 2 * m)
            add(("proj", m, 1, j), None, 0, [("norm", j)] + theirs(m), 43 + 20 * j + 2 * m)
        for cc in range(2):
            for q in range(2):
                add(("attn", q, cc, j), None, 0,
                    [("bias",)] + [("proj", m, cc, j) for m in range(3)], 48 + 20 * j)
        for n, step in enumerate((2, 1, 3, 0)):
            add(("out", step, j), None, 0,
                [("attn", q, cc, j) for q in range(2) for cc in range(2)] + mine(3) + theirs(3),
                50 + 20 * j + n)
        for d in "+-":
            for r in range(4):
                for hh in range(2):
                    first = (hh == 0) == (d == "+")
                    if r == 0 and not first:
                        continue
                    steps = {0: (2,), 1: (2, 1, 3), 2: (1, 3, 2), 3: (0, 1, 2, 3)}[r]
                    need = [("out", step, j) for step in steps]
                    if r >= 2 or (r == 1 and first):
                        need.append(("R", d, r - 1, hh, j))
                    add(("R", d, r, hh, j), "z" + d, 128, need, 30 + 20 * j - r)
        for hh in (1, 0):
            add(("fin", hh, j), "d" if hh else None, 128,
                [("out", 0, j), ("R", "+", 3, hh, j), ("R", "-", 3, hh, j)], 30 + j)
    return tasks


def list_schedule():
    tasks = make_tasks()
    free = dict.fromkeys(LINKS, 0.0)
    arrive, finished, order = {}, {}, []
    left = dict(tasks)
    now = 0.0

    def ready_at(tid):
        t = 0.0
        for n in tasks[tid][2]:
            when = arrive.get(n) if tasks[n][0] else finished.get(n)
            if when is None:
                return None
            t = max(t, when)
        return t

    while left:
        best, soonest = None, None
        for tid in left:
            link, kib, _, rank = tasks[tid]
            at = ready_at(tid)
            if at is None:
                continue
            links = ("z+", "z-") if link == "z" else (link,) if link else ()
            for one in links:
                at = max(at, free[one] - AHEAD)
            if at <= now + 1e-9:
                key = (0 if link else 1, rank, str(tid))
                if best is None or key < best[0]:
                    best = (key, tid, links)
            elif soonest is None or at < soonest:
                soonest = at
        if best is None:
            now = soonest
            continue
        _, tid, links = best
        link, kib, _, _ = tasks[tid]
        kind = {"R": "rs"}.get(tid[0], tid[0])
        now += COST.get(kind, 0.06)
        finished[tid] = now
        if link:
            rate = RATE.get(link, 46.6e3) / 1.024e3
            t = max([now] + [free[one] for one in links]) + kib / rate
            for one in links:
                free[one] = t
            arrive[tid] = t + (1.0 if link == "d" else 1.8)
        order.append(tid)
        del left[tid]
    return tasks, order, finished, arrive


def kernel(x_ref, g_ref, w_ref, pb_ref, mk_ref, o_ref,
           wb, hb, nb, qkv, att, ob, sb, rb, bt, pbs, mks, fs, fr,
           loc_sem, send_sem, hr, hd, wzs, wf, wf2, ws, ws2, wd, rr, sm, fin):
    dp = lax.axis_index("dp")
    mp = lax.axis_index("mp")
    zl, xi, yi = dp // 16, (dp // 4) % 4, dp % 4
    zh, c = mp // 2, mp % 2
    z = zh * 2 + zl
    oc = 1 - c
    oz = 1 - zl

    def dev(zz, xx, yy, cc):
        return ((zz % 2) * 16 + xx * 4 + yy, (zz // 2) * 2 + cc)

    xp, xm = (xi + 1) % 4, (xi + 3) % 4
    yp, ym = (yi + 1) % 4, (yi + 3) % 4
    devices = {
        "x+": dev(z, xp, yi, c), "x-": dev(z, xm, yi, c),
        "y+": dev(z, xi, yp, c), "y-": dev(z, xi, ym, c),
        "z+": dev((z + 1) % 8, xi, yi, c), "z-": dev((z + 7) % 8, xi, yi, c),
        "d": dev(z, xi, yi, oc), "z": dev(zh * 2 + oz, xi, yi, c),
    }
    pending = []

    def send(src, dst, sem, link):
        d = pltpu.make_async_remote_copy(
            src_ref=src, dst_ref=dst, send_sem=send_sem.at[0], recv_sem=sem,
            device_id=devices[link], device_id_type=MESH)
        d.start()
        pending.append(d)

    def recv(dst, sem):
        pltpu.make_async_remote_copy(
            src_ref=dst, dst_ref=dst, send_sem=send_sem.at[0], recv_sem=sem,
            device_id=devices["d"], device_id_type=MESH).wait_recv()

    barrier = pltpu.get_barrier_semaphore()
    for link in LINKS:
        pl.semaphore_signal(barrier, inc=1, device_id=devices[link], device_id_type=MESH)
    pl.semaphore_wait(barrier, len(LINKS))

    def blk(m, cls, f, s):
        bx, by = (f, s) if cls == 0 else (s, f)
        return wb.at[m, c, zl if cls == 0 else oz, bx, by]

    def axes(cls):
        return ("x", "y", xi, yi) if cls == 0 else ("y", "x", yi, xi)

    def step(i, d):
        return (i + (1 if d == "+" else 3)) % 4

    def fblock(cls, o):
        f = axes(cls)[2]
        return (f + (0, 3, 1, 2)[o]) % 4

    def dslice(m, cls, ff, cc):
        if cls == 0:
            return wb.at[m, cc, zl, ff]
        return wb.at[m, cc, oz, :, ff]

    def col(zz, hh):
        return (zz // 2) * 2 + (c if hh == 0 else oc)

    def rows(zz, j):
        return pl.ds(pl.multiple_of((j * 2 + zz % 2) * LEN, LEN), LEN)

    def hpiece(zo, hh, j):
        return hb.at[col(zo, hh), rows(zo, j)]

    def side(d):
        return 0 if d == "+" else 1

    def issue(t):
        kind = t[0]
        if kind == "HD":
            send(x_ref.at[pl.ds((oc * 2 + t[1]) * LEN, LEN)], hb.at[mp, rows(z, t[1])], hd.at[t[1]], "d")
        elif kind == "ZX":
            send(w_ref.at[oz, t[1]], wb.at[t[1], c, zl, xi, yi], wzs.at[t[1]], "z")
        elif kind == "H":
            _, d, r, hh, j = t
            zo = (z + 8 - r) % 8 if d == "+" else (z + r) % 8
            p = hpiece(zo, hh, j)
            send(p, p, hr.at[side(d), r, hh, j], "z" + d)
        elif kind == "F":
            _, cls, m, d = t
            fa, sa, f, s = axes(cls)
            own = blk(m, cls, f, s)
            send(w_ref.at[zl, m] if cls == 0 else own, own, wf.at[cls, m, side(d)], fa + d)
        elif kind == "F2":
            _, cls, m = t
            fa, sa, f, s = axes(cls)
            d = "+-"[(m + cls) % 2]
            b = blk(m, cls, step(f, flip(d)), s)
            send(b, b, wf2.at[cls, m], fa + d)
        elif kind == "S":
            _, cls, m, o, d = t
            fa, sa, f, s = axes(cls)
            b = blk(m, cls, fblock(cls, o), s)
            send(w_ref.at[zl, m] if cls == 0 and o == 0 else b, b, ws.at[cls, m, o, side(d)], sa + d)
        elif kind == "S2":
            _, cls, m, o = t
            fa, sa, f, s = axes(cls)
            d = "+-"[(m + cls + o) % 2]
            b = blk(m, cls, fblock(cls, o), step(s, flip(d)))
            send(b, b, ws2.at[cls, m, o], sa + d)
        elif kind == "D":
            _, cls, m, o = t
            p = dslice(m, cls, fblock(cls, o), c)
            send(p, p, wd.at[cls, m, o], "d")
        elif kind == "R":
            _, d, r, hh, j = t
            first = (hh == 0) == (d == "+")
            dz = (z + 4 - r) % 8 if d == "+" else (z + 4 + r) % 8
            value = ob[col(dz, hh), rows(dz, j), :]
            if r >= 2 or (r == 1 and first):
                value = value + rb[side(d), r - 1, hh, j].astype(F32)
            sb[side(d), r, hh, j] = value.astype(BF16)
            send(sb.at[side(d), r, hh, j], rb.at[side(d), r, hh, j], rr.at[side(d), r, hh, j], "z" + d)
        elif kind == "fin":
            _, hh, j = t
            value = (hb[col(z, hh), rows(z, j), :].astype(F32) + ob[col(z, hh), rows(z, j), :]
                     + rb[0, 3, hh, j].astype(F32) + rb[1, 3, hh, j].astype(F32)).astype(BF16)
            if hh:
                fs[j] = value
                send(fs.at[j], fr.at[j], fin.at[j], "d")
            else:
                o_ref[pl.ds((c * 2 + j) * LEN, LEN), :] = value
        elif kind == "bias":
            bias()
        elif kind == "norm":
            norm(t[1])
        elif kind == "proj":
            _, m, cc, j = t
            who = c if cc == 0 else oc
            w = wb[m, who].reshape(4096, 256)
            half = slice(j * 256, j * 256 + 256)
            qkv[m, who, half, :] = jnp.dot(
                nb[half, :], w, preferred_element_type=F32).astype(BF16)
        elif kind == "attn":
            attend(*t[1:])
        elif kind == "out":
            zq = (zh + t[1]) % 4
            half = slice(t[2] * 256, t[2] * 256 + 256)
            for hh in range(2):
                fb = zq * 2 + hh
                total = None
                for cc in range(2):
                    w = wb[3, cc, fb // 4, fb % 4].reshape(512, 256)
                    part = lax.dot_general(att[cc, half, :], w, NT, preferred_element_type=F32)
                    total = part if total is None else total + part
                ob[fb, half, :] = total

    def land(t):
        kind = t[0]
        if kind == "HD":
            recv(hb.at[zh * 2 + oc, rows(z, t[1])], hd.at[t[1]])
        elif kind == "ZX":
            recv(blk(t[1], 1, yi, xi), wzs.at[t[1]])
        elif kind == "H":
            _, d, r, hh, j = t
            zo = (z + 7 - r) % 8 if d == "+" else (z + 1 + r) % 8
            recv(hpiece(zo, hh, j), hr.at[side(d), r, hh, j])
        elif kind == "F":
            _, cls, m, d = t
            fa, sa, f, s = axes(cls)
            recv(blk(m, cls, step(f, flip(d)), s), wf.at[cls, m, side(d)])
        elif kind == "F2":
            _, cls, m = t
            fa, sa, f, s = axes(cls)
            recv(blk(m, cls, (f + 2) % 4, s), wf2.at[cls, m])
        elif kind == "S":
            _, cls, m, o, d = t
            fa, sa, f, s = axes(cls)
            recv(blk(m, cls, fblock(cls, o), step(s, flip(d))), ws.at[cls, m, o, side(d)])
        elif kind == "S2":
            _, cls, m, o = t
            fa, sa, f, s = axes(cls)
            recv(blk(m, cls, fblock(cls, o), (s + 2) % 4), ws2.at[cls, m, o])
        elif kind == "D":
            _, cls, m, o = t
            recv(dslice(m, cls, fblock(cls, o), oc), wd.at[cls, m, o])
        elif kind == "R":
            _, d, r, hh, j = t
            recv(rb.at[side(d), r, hh, j], rr.at[side(d), r, hh, j])

    def bias():
        recv(pbs.at[oc], sm.at[0])
        recv(mks.at[oz], sm.at[1])
        row = lax.broadcasted_iota(jnp.int32, (LEN, LEN), 0)
        lane = lax.broadcasted_iota(jnp.int32, (LEN, LEN), 1)
        rel = lane - row
        dist = jnp.abs(rel)
        bucket = jnp.where(rel > 0, BUCKETS // 2, 0)
        for t in STEPS:
            bucket = bucket + jnp.where(dist >= t, 1, 0)

        def bias_head(i, _):
            cc, h = i // 4, i % 4
            tab = jnp.zeros((LEN, LEN), F32)
            for b in range(BUCKETS):
                tab = jnp.where(bucket == b, pbs[cc, h, pl.ds(b, 1), :], tab)
            bt[cc, pl.ds(pl.multiple_of(h * LEN, LEN), LEN), :] = tab
            return 0

        lax.fori_loop(0, 8, bias_head, 0)

    def norm(j):
        def norm_rows(i, _):
            at = pl.ds(pl.multiple_of(i * 16, 16), 16)
            total = jnp.zeros((16, 512), F32)
            for fb in range(8):
                v = hb[fb, at, :].astype(F32)
                total = total + v * v
            ms = jnp.sum(total, axis=-1, keepdims=True) * (1.0 / 4096.0)
            scale = lax.rsqrt(ms + EPS)
            for fb in range(8):
                v = hb[fb, at, :].astype(F32)
                nb[at, fb * 512:(fb + 1) * 512] = (
                    v * scale * g_ref[:, fb * 512:(fb + 1) * 512]).astype(BF16)
            return 0

        lax.fori_loop(j * 16, j * 16 + 16, norm_rows, 0)

    def attend(q, cc, j):
        head = lax.broadcasted_iota(jnp.int32, (LEN, 256), 1) // DH
        who = c if cc == 0 else oc
        at = slice((j * 2 + q) * LEN, (j * 2 + q + 1) * LEN)
        qq, kk, v = qkv[0, who, at, :], qkv[1, who, at, :], qkv[2, who, at, :]
        zero = jnp.zeros((), BF16)
        qm = jnp.concatenate([jnp.where(head == h, qq, zero) for h in range(4)], axis=0)
        s = lax.dot_general(qm, kk, NT, preferred_element_type=F32) + bt[who]
        seen = mks[q, pl.ds(2 * c + j, 1), :]
        s = jnp.where(seen > 0.5, s, -1e30)
        top = jnp.max(s, axis=-1, keepdims=True)
        e = jnp.exp(s - top)
        w = (e / jnp.sum(e, axis=-1, keepdims=True)).astype(BF16)
        mix = jnp.dot(w, v, preferred_element_type=F32)
        out = jnp.zeros((LEN, 256), F32)
        for h in range(4):
            out = jnp.where(head == h, mix[h * LEN:(h + 1) * LEN], out)
        att[who, at, :] = out.astype(BF16)

    locs = []
    for j in range(2):
        locs.append(pltpu.make_async_copy(
            x_ref.at[pl.ds((c * 2 + j) * LEN, LEN)], hb.at[mp, rows(z, j)], loc_sem.at[j]))
    for m in range(4):
        locs.append(pltpu.make_async_copy(w_ref.at[zl, m], blk(m, 0, xi, yi), loc_sem.at[2 + m]))
    locs.append(pltpu.make_async_copy(pb_ref.at[pl.ds(zl * 4, 4)], pbs.at[c], loc_sem.at[6]))
    locs.append(pltpu.make_async_copy(mk_ref, mks.at[zl], loc_sem.at[7]))
    for d in locs:
        d.start()
    send(pb_ref.at[pl.ds(zl * 4, 4)], pbs.at[c], sm.at[0], "d")
    send(mk_ref, mks.at[zl], sm.at[1], "z")
    for d in locs:
        d.wait()

    tasks, order, _, _ = list_schedule()
    landed = set()
    for t in order:
        for n in tasks[t][2]:
            if tasks[n][0] and n not in landed:
                land(n)
                landed.add(n)
        issue(t)
    for t in order:
        if tasks[t][0] and t[0] != "fin" and t not in landed:
            land(t)
    for j in range(2):
        recv(fr.at[j], fin.at[j])
        o_ref[pl.ds((oc * 2 + j) * LEN, LEN), :] = fr[j]
    for d in pending:
        d.wait_send()


def local(hidden_states, norm_gain, query_weight, keyvalue_weight, output_weight,
          position_bias, lengths):
    kv = jnp.transpose(keyvalue_weight[0], (1, 0, 2))
    w = jnp.stack([query_weight[0], kv[0], kv[1], output_weight[0]])
    w = jnp.transpose(w.reshape(4, 128, 2, 256), (2, 0, 1, 3))
    pb = jnp.broadcast_to(jnp.transpose(position_bias[0])[:, :, None], (8, BUCKETS, LEN))
    mask = (jnp.arange(LEN)[None, :] < lengths[:, None]).astype(F32)
    mask = jnp.concatenate([mask, jnp.zeros((4, LEN), F32)])
    vm = pl.BlockSpec(memory_space=pltpu.VMEM)
    dma = pltpu.SemaphoreType.DMA
    return pl.pallas_call(
        kernel,
        out_shape=jax.ShapeDtypeStruct((512, 512), BF16),
        in_specs=[vm] * 5,
        out_specs=vm,
        scratch_shapes=[
            pltpu.VMEM((4, 2, 2, 4, 4, 128, 256), BF16),
            pltpu.VMEM((8, 512, 512), BF16),
            pltpu.VMEM((512, 4096), BF16),
            pltpu.VMEM((3, 2, 512, 256), BF16),
            pltpu.VMEM((2, 512, 256), BF16),
            pltpu.VMEM((8, 512, 512), F32),
            pltpu.VMEM((2, 4, 2, 2, 128, 512), BF16),
            pltpu.VMEM((2, 4, 2, 2, 128, 512), BF16),
            pltpu.VMEM((2, 512, 128), F32),
            pltpu.VMEM((2, 4, BUCKETS, LEN), F32),
            pltpu.VMEM((2, 8, LEN), F32),
            pltpu.VMEM((2, 128, 512), BF16),
            pltpu.VMEM((2, 128, 512), BF16),
            dma((8,)),
            dma((1,)),
            dma((2, 4, 2, 2)),
            dma((2,)),
            dma((4,)),
            dma((2, 4, 2)),
            dma((2, 4)),
            dma((2, 4, 4, 2)),
            dma((2, 4, 4)),
            dma((2, 4, 4)),
            dma((2, 4, 2, 2)),
            dma((2,)),
            dma((2,)),
        ],
        compiler_params=pltpu.CompilerParams(
            collective_id=0, has_side_effects=True, vmem_limit_bytes=60 * 1024 * 1024),
        name="t5_attention",
    )(hidden_states, norm_gain, w, pb, mask)


def solution(mesh):
    in_specs = (
        P("dp", "mp"),
        P(),
        P(None, "dp", "mp"),
        P(None, "dp", None, "mp"),
        P(None, "dp", "mp"),
        P(None, None, "mp"),
        P("dp"),
    )
    return jax.shard_map(local, mesh=mesh, in_specs=in_specs, out_specs=P("dp", "mp"), check_vma=False)
```

time: 413 us -> 117 us (0.28)
  waiting for transfers between devices: 354 us -> 0 us
  Pallas kernels: 0 us -> 110 us
  matrix products: 25.4 us -> 0 us
  between operations: 13.2 us -> 0.07 us
  local copies, waits for them, and re-layouts: 12.6 us -> 5.75 us
  other arithmetic: 6 us -> 0.73 us
    all_gather x2 -> x0, waiting for transfers between devices: 276 us -> none  [the longest x1 223 us: side_by_side(): filled, at, outs = (lax.all_gather(both, axis, axis=dim, tiled=True), 0, [])]
    pallas_call x0 -> x1, Pallas kernels: none -> 110 us  [local(): pl.pallas_call(kernel, out_shape=jax.ShapeDtypeStruct((512, 512), BF16),...]
    reduce_scatter x1 -> x0, waiting for transfers between devices: 77.3 us -> none  [local(): lax.psum_scatter(partial_out.astype(jnp.bfloat16), 'mp', scatter_dimensio...]
    dot_general x5 -> x0, matrix products: 22.9 us -> none  [the longest x1 7.31 us: add_projections(): jnp.einsum('td,dcf->ctf', normed, pair_piece, preferred_element_type=jnp....]
    slice x2 -> x0, local copies, waits for them, and re-layouts: 7.94 us -> none  [the longest x1 7.87 us: side_by_side(): piece = filled[..., at:at + column.shape[along]]]
  transfers between devices with their start and end apart: 3 -> 0, of which waited for: 3 -> 0; matrix products, arithmetic and copies ran while one was open for 2% -> 0% of each run, Pallas kernels for 0% -> 0%
where the time goes in v2:
time: 117 us
  Pallas kernels  110 us (94%)
  local copies, waits for them, and re-layouts  5.75 us (5%)
    pallas_call x1, Pallas kernels, local(): pl.pallas_call(kernel, out_shape=jax.ShapeDtypeStruct((512, 512), BF16),...  110 us
    unnamed x12, local copies, waits for them, and re-layouts  4 us

profile of v2, /device:TPU:1, one launch (start us, length us, event | category | flops | bytes accessed | tf_op | source)
XLA Modules:
  0.0 116.8 jit_solution(7206254145609411253)
XLA Ops:
  0.0 0.0 copy-start.3
  0.0 0.7 copy-done.3
  0.7 0.1 iota_compare_fusion
  0.7 0.6 pad_convert_fusion.mk_ref
  1.3 0.0 copy-start.1
  1.3 0.0 copy-start.2
  1.3 1.1 copy.11
  2.4 0.0 copy-done.1
  2.4 0.0 copy-start
  2.4 0.1 copy.12
  2.5 0.0 copy-done.2
  2.5 0.7 broadcast_in_dim.2.pb_ref
  3.3 0.1 copy-done
  3.4 0.2 copy.10
  3.6 0.1 pad_maximum_fusion
  3.7 1.0 copy.13
  4.7 110.2 %t5_attention.1 = bf16[512,512]{1,0:T(8,128)(2,1)} custom-call(bf16[512,512]{1,0:T(8,128)(2,1)} %x_ref.1, f32[1,4096]{1,0:T(1,128)} %g_ref.1, bf16[2,4,128,256]{3,2,1,0:T(8,128)(2,1)} %bitcast.9, f32[8,32,128]{2,1,0:T(8,128)} %broadcast_in_dim.2.pb_ref, f32[8,128]{1,0:T(8,128)} %pad_convert_fusion.mk_ref), custom_call_target="tpu_custom_call" | custom-call | tf_op jit(solution)/shard_map/t5_attention/pallas_call | solution.py:461
  114.9 1.9 %copy.15 = bf16[512,512]{1,0:T(8,128)(2,1)} copy(bf16[512,512]{1,0:T(8,128)(2,1)} %t5_attention.1) | data formatting | bytes 1048576
Async XLA Ops:
  0.0 0.7 copy-start.3
  1.3 1.1 copy-start.1
  1.3 1.2 %copy-start.2 = (f32[1,32,8]{1,2,0:T(8,128)S(1)}, f32[1,32,8]{1,2,0:T(8,128)}, u32[]{:S(2)}) copy-start(f32[1,32,8]{1,2,0:T(8,128)} %param.12) | copy-start | bytes 3076
  2.4 1.0 copy-start

commit v3 on v2

--- a/solution.py
+++ b/solution.py
@@ -32,14 +32,30 @@
 STEPS = far_steps()
 
 
-LINKS = ("x+", "x-", "y+", "y-", "z+", "z-", "d")
+LINKS = ("x+", "x-", "y+", "y-", "zp", "zn", "d")
 RATE = {"d": 400e3}
-COST = {"norm": 1.0, "proj": 0.9, "attn": 0.55, "out": 0.5, "bias": 2.2, "rs": 0.25, "fin": 0.4}
+COST = {"norm": 1.2, "proj": 0.65, "attn": 0.35, "out": 0.4, "bias": 1.6, "rs": 0.2, "fin": 0.3,
+        "prep": 1.0, "small": 0.4}
 AHEAD = 3.0
 
 
+H_HOPS = {(0, 0): 4, (1, 0): 3, (0, 1): 4, (1, 1): 3}
+R_HOPS = {(0, 0): 4, (1, 0): 3, (0, 1): 4, (1, 1): 3}
+
+
 def flip(d):
-    return "-" if d == "+" else "+"
+    return {"+": "-", "-": "+", "p": "n", "n": "p"}[d]
+
+
+def rounds(hops, d, r):
+    side = d if r % 2 == 0 else flip(d)
+    return hops if side == "p" else 7 - hops
+
+
+OUT_NEED = {("p", 0): ("own",), ("p", 1): ("p",), ("p", 2): ("p",), ("p", 3): ("far",),
+            ("n", 0): ("n",), ("n", 1): ("n",), ("n", 2): ("far",), ("n", 3): ("far",)}
+RANK = {"zx": (-14.4, 33.6, 2.8, 33.7), "h": (18.2, 34.9), "w": (4.1, 4.4, -0.5, 13.9), "f": -6.4, "s0": -19.3, "s1": 0.0,
+        "s3": 9.7, "f2": -21.4, "s2": -5.3, "r": 58.5}
 
 
 def make_tasks():
@@ -48,38 +64,41 @@
     def add(tid, link, kib, needs, rank):
         tasks[tid] = (link, kib, tuple(needs), rank)
 
+    add(("prep",), None, 0, (), 0.2)
+    add(("small",), None, 0, [("prep",)], 30)
     for j in range(2):
         add(("HD", j), "d", 128, (), 0)
     for m in range(4):
-        add(("ZX", m), "z", 64, (), 0.5 if m < 3 else 14)
+        add(("ZX", m), "zp", 64, [("prep",)] if m in (1, 2) else (), RANK["zx"][m])
     for j in range(2):
-        for d in "+-":
+        for d in "pn":
             for r in range(4):
                 for hh in range(2):
-                    if r == 3 and (hh == 0) != (d == "+"):
+                    if r >= rounds(H_HOPS[hh, j], d, r):
                         continue
                     need = [("HD", j)] if r == 0 and hh == 1 else []
                     if r > 0:
-                        need = [("H", d, r - 1, hh, j)]
-                    add(("H", d, r, hh, j), "z" + d, 128, need, 1 + 20 * j + r)
+                        need = [("H", flip(d), r - 1, hh, j)]
+                    add(("H", d, r, hh, j), "z" + d, 128, need, RANK["h"][j] + r)
     for m in range(4):
-        late = 10 if m == 3 else 0
+        late = RANK["w"][m]
         for cls in range(2):
             fa, sa = ("x", "y") if cls == 0 else ("y", "x")
-            base = [("ZX", m)] if cls else []
+            base = [("ZX", m)] if cls else [("prep",)] if m in (1, 2) else []
             for d in "+-":
-                add(("F", cls, m, d), fa + d, 64, base, m + late)
-                add(("S", cls, m, 0, d), sa + d, 64, base, m + late + 1)
-                add(("S", cls, m, 1, d), sa + d, 64, [("F", cls, m, "+")], m + late + 1)
-                add(("S", cls, m, 2, d), sa + d, 64, [("F", cls, m, "-")], m + late + 1)
-                add(("S", cls, m, 3, d), sa + d, 64, [("F2", cls, m)], m + late)
+                add(("F", cls, m, d), fa + d, 64, base, late + RANK["f"])
+                add(("S", cls, m, 0, d), sa + d, 64, base, late + RANK["s0"])
+                add(("S", cls, m, 1, d), sa + d, 64, [("F", cls, m, "+")], late + RANK["s1"])
+                add(("S", cls, m, 2, d), sa + d, 64, [("F", cls, m, "-")], late + RANK["s1"])
+                add(("S", cls, m, 3, d), sa + d, 64, [("F2", cls, m)], late + RANK["s3"])
             d = "+-"[(m + cls) % 2]
-            add(("F2", cls, m), fa + d, 64, [("F", cls, m, d)], m + late - 1)
+            add(("F2", cls, m), fa + d, 64, [("F", cls, m, d)], late + RANK["f2"])
             for o in range(4):
                 d = "+-"[(m + cls + o) % 2]
-                add(("S2", cls, m, o), sa + d, 64, [("S", cls, m, o, d)], m + late + 0.5)
+                add(("S2", cls, m, o), sa + d, 64, [("S", cls, m, o, d)], late + RANK["s2"])
                 add(("D", cls, m, o), "d", 256,
-                    [("S", cls, m, o, "+"), ("S", cls, m, o, "-"), ("S2", cls, m, o)], m + late)
+                    [("S", cls, m, o, "+"), ("S", cls, m, o, "-"), ("S2", cls, m, o)]
+                    + ([("small",)] if o == 0 else []), late)
 
     def mine(m):
         return ([("ZX", m)] + [("F", c, m, d) for c in range(2) for d in "+-"]
@@ -90,35 +109,34 @@
     def theirs(m):
         return [("D", c, m, o) for c in range(2) for o in range(4)]
 
-    add(("bias",), None, 0, (), 60)
+    add(("bias",), None, 0, [("small",)], 60)
     for j in range(2):
         add(("norm", j), None, 0,
             [("HD", j)] + [t for t in tasks if t[0] == "H" and t[4] == j], 40 + j)
         for m in range(3):
-            add(("proj", m, 0, j), None, 0, [("norm", j)] + mine(m), 42 + 20 * j + 2 * m)
+            add(("proj", m, 0, j), None, 0, [("norm", j), ("small",)] + mine(m), 42 + 20 * j + 2 * m)
             add(("proj", m, 1, j), None, 0, [("norm", j)] + theirs(m), 43 + 20 * j + 2 * m)
         for cc in range(2):
             for q in range(2):
                 add(("attn", q, cc, j), None, 0,
                     [("bias",)] + [("proj", m, cc, j) for m in range(3)], 48 + 20 * j)
-        for n, step in enumerate((2, 1, 3, 0)):
+        for n, step in enumerate(("far", "n", "p", "own")):
             add(("out", step, j), None, 0,
                 [("attn", q, cc, j) for q in range(2) for cc in range(2)] + mine(3) + theirs(3),
                 50 + 20 * j + n)
-        for d in "+-":
+        for d in "pn":
             for r in range(4):
                 for hh in range(2):
-                    first = (hh == 0) == (d == "+")
-                    if r == 0 and not first:
+                    hops = rounds(R_HOPS[hh, j], d, r)
+                    if r >= hops:
                         continue
-                    steps = {0: (2,), 1: (2, 1, 3), 2: (1, 3, 2), 3: (0, 1, 2, 3)}[r]
-                    need = [("out", step, j) for step in steps]
-                    if r >= 2 or (r == 1 and first):
-                        need.append(("R", d, r - 1, hh, j))
-                    add(("R", d, r, hh, j), "z" + d, 128, need, 30 + 20 * j - r)
+                    need = [("out", step, j) for step in (OUT_NEED[d, r])]
+                    if r < hops - 1:
+                        need.append(("R", flip(d), r + 1, hh, j))
+                    add(("R", d, r, hh, j), "z" + d, 128, need, 33 + RANK["r"] * j - r)
         for hh in (1, 0):
             add(("fin", hh, j), "d" if hh else None, 128,
-                [("out", 0, j), ("R", "+", 3, hh, j), ("R", "-", 3, hh, j)], 30 + j)
+                [("out", "own", j), ("R", "p", 0, hh, j), ("R", "n", 0, hh, j)], 30 + j)
     return tasks
 
 
@@ -145,7 +163,7 @@
             at = ready_at(tid)
             if at is None:
                 continue
-            links = ("z+", "z-") if link == "z" else (link,) if link else ()
+            links = (link,) if link else ()
             for one in links:
                 at = max(at, free[one] - AHEAD)
             if at <= now + 1e-9:
@@ -163,7 +181,7 @@
         now += COST.get(kind, 0.06)
         finished[tid] = now
         if link:
-            rate = RATE.get(link, 46.6e3) / 1.024e3
+            rate = RATE.get(link, 44.0e3) / 1.024e3
             t = max([now] + [free[one] for one in links]) + kib / rate
             for one in links:
                 free[one] = t
@@ -173,8 +191,9 @@
     return tasks, order, finished, arrive
 
 
-def kernel(x_ref, g_ref, w_ref, pb_ref, mk_ref, o_ref,
+def kernel(x_ref, g_hbm, q_hbm, kv_hbm, ow_hbm, pb_hbm, len_hbm, o_ref,
            wb, hb, nb, qkv, att, ob, sb, rb, bt, pbs, mks, fs, fr,
+           wq, wo, wkv, kvs, g_ref, pbv, lens,
            loc_sem, send_sem, hr, hd, wzs, wf, wf2, ws, ws2, wd, rr, sm, fin):
     dp = lax.axis_index("dp")
     mp = lax.axis_index("mp")
@@ -184,6 +203,11 @@
     oc = 1 - c
     oz = 1 - zl
 
+    toward = 1 - 2 * zl
+
+    def zstep(d, n):
+        return (z + 8 + (toward if d == "p" else -toward) * n) % 8
+
     def dev(zz, xx, yy, cc):
         return ((zz % 2) * 16 + xx * 4 + yy, (zz // 2) * 2 + cc)
 
@@ -192,8 +216,8 @@
     devices = {
         "x+": dev(z, xp, yi, c), "x-": dev(z, xm, yi, c),
         "y+": dev(z, xi, yp, c), "y-": dev(z, xi, ym, c),
-        "z+": dev((z + 1) % 8, xi, yi, c), "z-": dev((z + 7) % 8, xi, yi, c),
-        "d": dev(z, xi, yi, oc), "z": dev(zh * 2 + oz, xi, yi, c),
+        "zp": dev(zstep("p", 1), xi, yi, c), "zn": dev(zstep("n", 1), xi, yi, c),
+        "d": dev(z, xi, yi, oc),
     }
     pending = []
 
@@ -209,6 +233,35 @@
             src_ref=dst, dst_ref=dst, send_sem=send_sem.at[0], recv_sem=sem,
             device_id=devices["d"], device_id_type=MESH).wait_recv()
 
+    lanes = pl.ds(pl.multiple_of(zl * 256, 256), 256)
+    far_lanes = pl.ds(pl.multiple_of(oz * 256, 256), 256)
+
+    def source(m, at):
+        if m == 0:
+            return wq.at[:, at]
+        if m == 3:
+            return wo.at[:, at]
+        return kvs.at[m - 1, :, at]
+
+    def col(zz, hh):
+        return (zz // 2) * 2 + (c if hh == 0 else oc)
+
+    def rows(zz, j):
+        return pl.ds(pl.multiple_of((j * 2 + zz % 2) * LEN, LEN), LEN)
+
+    def local(i, src, dst):
+        d = pltpu.make_async_copy(src, dst, loc_sem.at[i])
+        d.start()
+        return d
+
+    own_x = [local(j, x_ref.at[pl.ds((c * 2 + j) * LEN, LEN)], hb.at[mp, rows(z, j)]) for j in range(2)]
+    own_q = local(2, q_hbm, wq)
+    own_kv = local(3, kv_hbm, wkv)
+    own_o = local(4, ow_hbm, wo)
+    rest = [local(5, pb_hbm, pbv), local(6, len_hbm, lens), local(7, g_hbm, g_ref),
+            local(8, q_hbm.at[:, lanes], wb.at[0, c, zl, xi, yi]),
+            local(9, ow_hbm.at[:, lanes], wb.at[3, c, zl, xi, yi])]
+
     barrier = pltpu.get_barrier_semaphore()
     for link in LINKS:
         pl.semaphore_signal(barrier, inc=1, device_id=devices[link], device_id_type=MESH)
@@ -233,34 +286,39 @@
             return wb.at[m, cc, zl, ff]
         return wb.at[m, cc, oz, :, ff]
 
-    def col(zz, hh):
-        return (zz // 2) * 2 + (c if hh == 0 else oc)
-
-    def rows(zz, j):
-        return pl.ds(pl.multiple_of((j * 2 + zz % 2) * LEN, LEN), LEN)
-
     def hpiece(zo, hh, j):
         return hb.at[col(zo, hh), rows(zo, j)]
 
     def side(d):
-        return 0 if d == "+" else 1
+        return 0 if d in "+p" else 1
+
+    waits = {"x0": own_x[0], "x1": own_x[1], "q": own_q, "o": own_o}
+
+    def gate(t):
+        key = None
+        if t[0] == "H" and t[2] == 0 and t[3] == 0:
+            key = "x%d" % t[4]
+        elif t[0] in ("ZX", "F", "S"):
+            m = t[1] if t[0] == "ZX" else t[2]
+            key = {0: "q", 3: "o"}.get(m)
+        if key in waits:
+            waits.pop(key).wait()
 
     def issue(t):
         kind = t[0]
         if kind == "HD":
             send(x_ref.at[pl.ds((oc * 2 + t[1]) * LEN, LEN)], hb.at[mp, rows(z, t[1])], hd.at[t[1]], "d")
         elif kind == "ZX":
-            send(w_ref.at[oz, t[1]], wb.at[t[1], c, zl, xi, yi], wzs.at[t[1]], "z")
+            send(source(t[1], far_lanes), wb.at[t[1], c, zl, xi, yi], wzs.at[t[1]], "zp")
         elif kind == "H":
             _, d, r, hh, j = t
-            zo = (z + 8 - r) % 8 if d == "+" else (z + r) % 8
-            p = hpiece(zo, hh, j)
+            p = hpiece(zstep(flip(d), r), hh, j)
             send(p, p, hr.at[side(d), r, hh, j], "z" + d)
         elif kind == "F":
             _, cls, m, d = t
             fa, sa, f, s = axes(cls)
             own = blk(m, cls, f, s)
-            send(w_ref.at[zl, m] if cls == 0 else own, own, wf.at[cls, m, side(d)], fa + d)
+            send(source(m, lanes) if cls == 0 else own, own, wf.at[cls, m, side(d)], fa + d)
         elif kind == "F2":
             _, cls, m = t
             fa, sa, f, s = axes(cls)
@@ -271,7 +329,7 @@
             _, cls, m, o, d = t
             fa, sa, f, s = axes(cls)
             b = blk(m, cls, fblock(cls, o), s)
-            send(w_ref.at[zl, m] if cls == 0 and o == 0 else b, b, ws.at[cls, m, o, side(d)], sa + d)
+            send(source(m, lanes) if cls == 0 and o == 0 else b, b, ws.at[cls, m, o, side(d)], sa + d)
         elif kind == "S2":
             _, cls, m, o = t
             fa, sa, f, s = axes(cls)
@@ -284,22 +342,25 @@
             send(p, p, wd.at[cls, m, o], "d")
         elif kind == "R":
             _, d, r, hh, j = t
-            first = (hh == 0) == (d == "+")
-            dz = (z + 4 - r) % 8 if d == "+" else (z + 4 + r) % 8
+            dz = zstep(d, r + 1)
             value = ob[col(dz, hh), rows(dz, j), :]
-            if r >= 2 or (r == 1 and first):
-                value = value + rb[side(d), r - 1, hh, j].astype(F32)
+            if r < rounds(R_HOPS[hh, j], d, r) - 1:
+                value = value + rb[side(flip(d)), r + 1, hh, j].astype(F32)
             sb[side(d), r, hh, j] = value.astype(BF16)
             send(sb.at[side(d), r, hh, j], rb.at[side(d), r, hh, j], rr.at[side(d), r, hh, j], "z" + d)
         elif kind == "fin":
             _, hh, j = t
             value = (hb[col(z, hh), rows(z, j), :].astype(F32) + ob[col(z, hh), rows(z, j), :]
-                     + rb[0, 3, hh, j].astype(F32) + rb[1, 3, hh, j].astype(F32)).astype(BF16)
+                     + rb[0, 0, hh, j].astype(F32) + rb[1, 0, hh, j].astype(F32)).astype(BF16)
             if hh:
                 fs[j] = value
                 send(fs.at[j], fr.at[j], fin.at[j], "d")
             else:
                 o_ref[pl.ds((c * 2 + j) * LEN, LEN), :] = value
+        elif kind == "prep":
+            prep()
+        elif kind == "small":
+            small()
         elif kind == "bias":
             bias()
         elif kind == "norm":
@@ -314,7 +375,7 @@
         elif kind == "attn":
             attend(*t[1:])
         elif kind == "out":
-            zq = (zh + t[1]) % 4
+            zq = {"own": zh, "p": zstep("p", 2) // 2, "n": zstep("n", 1) // 2, "far": (zh + 2) % 4}[t[1]]
             half = slice(t[2] * 256, t[2] * 256 + 256)
             for hh in range(2):
                 fb = zq * 2 + hh
@@ -333,8 +394,7 @@
             recv(blk(t[1], 1, yi, xi), wzs.at[t[1]])
         elif kind == "H":
             _, d, r, hh, j = t
-            zo = (z + 7 - r) % 8 if d == "+" else (z + 1 + r) % 8
-            recv(hpiece(zo, hh, j), hr.at[side(d), r, hh, j])
+            recv(hpiece(zstep(d, r + 1), hh, j), hr.at[side(d), r, hh, j])
         elif kind == "F":
             _, cls, m, d = t
             fa, sa, f, s = axes(cls)
@@ -357,6 +417,23 @@
         elif kind == "R":
             _, d, r, hh, j = t
             recv(rb.at[side(d), r, hh, j], rr.at[side(d), r, hh, j])
+
+    def prep():
+        own_kv.wait()
+        for i in range(2):
+            kvs[i] = wkv[:, i, :]
+            rest.append(local(10 + i, kvs.at[i, :, lanes], wb.at[1 + i, c, zl, xi, yi]))
+
+    def small():
+        for d in rest:
+            d.wait()
+        for b in range(BUCKETS):
+            pbs[c, b] = jnp.broadcast_to(pbv[:, b:b + 1], (8, LEN))
+        lane = lax.broadcasted_iota(jnp.int32, (1, LEN), 1)
+        for i in range(4):
+            mks[zl, pl.ds(i, 1), :] = jnp.where(lane < lens[i], 1.0, 0.0)
+        send(pbs.at[c], pbs.at[c], sm.at[0], "d")
+        send(mks.at[zl], mks.at[zl], sm.at[1], "zp")
 
     def bias():
         recv(pbs.at[oc], sm.at[0])
@@ -373,7 +450,7 @@
             cc, h = i // 4, i % 4
             tab = jnp.zeros((LEN, LEN), F32)
             for b in range(BUCKETS):
-                tab = jnp.where(bucket == b, pbs[cc, h, pl.ds(b, 1), :], tab)
+                tab = jnp.where(bucket == b, pbs[cc, b, pl.ds(zl * 4 + h, 1), :], tab)
             bt[cc, pl.ds(pl.multiple_of(h * LEN, LEN), LEN), :] = tab
             return 0
 
@@ -415,21 +492,6 @@
             out = jnp.where(head == h, mix[h * LEN:(h + 1) * LEN], out)
         att[who, at, :] = out.astype(BF16)
 
-    locs = []
-    for j in range(2):
-        locs.append(pltpu.make_async_copy(
-            x_ref.at[pl.ds((c * 2 + j) * LEN, LEN)], hb.at[mp, rows(z, j)], loc_sem.at[j]))
-    for m in range(4):
-        locs.append(pltpu.make_async_copy(w_ref.at[zl, m], blk(m, 0, xi, yi), loc_sem.at[2 + m]))
-    locs.append(pltpu.make_async_copy(pb_ref.at[pl.ds(zl * 4, 4)], pbs.at[c], loc_sem.at[6]))
-    locs.append(pltpu.make_async_copy(mk_ref, mks.at[zl], loc_sem.at[7]))
-    for d in locs:
-        d.start()
-    send(pb_ref.at[pl.ds(zl * 4, 4)], pbs.at[c], sm.at[0], "d")
-    send(mk_ref, mks.at[zl], sm.at[1], "z")
-    for d in locs:
-        d.wait()
-
     tasks, order, _, _ = list_schedule()
     landed = set()
     for t in order:
@@ -437,6 +499,7 @@
             if tasks[n][0] and n not in landed:
                 land(n)
                 landed.add(n)
+        gate(t)
         issue(t)
     for t in order:
         if tasks[t][0] and t[0] != "fin" and t not in landed:
@@ -450,18 +513,13 @@
 
 def local(hidden_states, norm_gain, query_weight, keyvalue_weight, output_weight,
           position_bias, lengths):
-    kv = jnp.transpose(keyvalue_weight[0], (1, 0, 2))
-    w = jnp.stack([query_weight[0], kv[0], kv[1], output_weight[0]])
-    w = jnp.transpose(w.reshape(4, 128, 2, 256), (2, 0, 1, 3))
-    pb = jnp.broadcast_to(jnp.transpose(position_bias[0])[:, :, None], (8, BUCKETS, LEN))
-    mask = (jnp.arange(LEN)[None, :] < lengths[:, None]).astype(F32)
-    mask = jnp.concatenate([mask, jnp.zeros((4, LEN), F32)])
     vm = pl.BlockSpec(memory_space=pltpu.VMEM)
+    hbm = pl.BlockSpec(memory_space=pl.ANY)
     dma = pltpu.SemaphoreType.DMA
     return pl.pallas_call(
         kernel,
         out_shape=jax.ShapeDtypeStruct((512, 512), BF16),
-        in_specs=[vm] * 5,
+        in_specs=[hbm] * 7,
         out_specs=vm,
         scratch_shapes=[
             pltpu.VMEM((4, 2, 2, 4, 4, 128, 256), BF16),
@@ -473,11 +531,18 @@
             pltpu.VMEM((2, 4, 2, 2, 128, 512), BF16),
             pltpu.VMEM((2, 4, 2, 2, 128, 512), BF16),
             pltpu.VMEM((2, 512, 128), F32),
-            pltpu.VMEM((2, 4, BUCKETS, LEN), F32),
+            pltpu.VMEM((2, BUCKETS, 8, LEN), F32),
             pltpu.VMEM((2, 8, LEN), F32),
             pltpu.VMEM((2, 128, 512), BF16),
             pltpu.VMEM((2, 128, 512), BF16),
-            dma((8,)),
+            pltpu.VMEM((128, 512), BF16),
+            pltpu.VMEM((128, 512), BF16),
+            pltpu.VMEM((128, 2, 512), BF16),
+            pltpu.VMEM((2, 128, 512), BF16),
+            pltpu.VMEM((1, 4096), F32),
+            pltpu.VMEM((8, BUCKETS), F32),
+            pltpu.SMEM((4,), jnp.int32),
+            dma((12,)),
             dma((1,)),
             dma((2, 4, 2, 2)),
             dma((2,)),
@@ -494,7 +559,8 @@
         compiler_params=pltpu.CompilerParams(
             collective_id=0, has_side_effects=True, vmem_limit_bytes=60 * 1024 * 1024),
         name="t5_attention",
-    )(hidden_states, norm_gain, w, pb, mask)
+    )(hidden_states, norm_gain, query_weight[0], keyvalue_weight[0], output_weight[0],
+      jnp.transpose(position_bias[0]), lengths)
 
 
 def solution(mesh):

time: 117 us -> 112 us (0.957)
  local copies, waits for them, and re-layouts: 5.75 us -> 1.87 us
    unnamed x12 -> x1, local copies, waits for them, and re-layouts: 4 us -> 1.87 us
where the time goes in v3:
time: 112 us; the launch traced here: 111 us
  Pallas kernels  110 us (98%)
  local copies, waits for them, and re-layouts  1.87 us (2%)
    pallas_call x1, Pallas kernels, local(): pl.pallas_call(kernel, out_shape=jax.ShapeDtypeStruct((512, 512), BF16),...  110 us

profile of v3, /device:TPU:1, one launch (start us, length us, event | category | flops | bytes accessed | tf_op | source)
XLA Modules:
  0.0 111.4 jit_solution(16971385606386477303)
XLA Ops:
  0.0 109.5 %t5_attention.1 = bf16[512,512]{1,0:T(8,128)(2,1)} custom-call(bf16[512,512]{1,0:T(8,128)(2,1)} %x_ref.1, f32[1,4096]{1,0:T(1,128)} %g_hbm.1, bf16[128,512]{1,0:T(8,128)(2,1)} %bitcast.7, bf16[128,2,512]{2,1,0:T(2,128)(2,1)} %bitcast.6, bf16[128,512]{1,0:T(8,128)(2,1)} %bitcast.8, f32[8,32]{1,0:T(8,128)} %bitcast.9, s32[4]{0:T(128)} %len_hbm.1), custom_call_target="tpu_custom_call" | custom-call | tf_op jit(solution)/shard_map/t5_attention/pallas_call | solution.py:519
  109.6 1.9 %copy.9 = bf16[512,512]{1,0:T(8,128)(2,1)} copy(bf16[512,512]{1,0:T(8,128)(2,1)} %t5_attention.1) | data formatting | bytes 1048576

commit v4 on v3

--- a/solution.py
+++ b/solution.py
@@ -34,12 +34,12 @@
 
 LINKS = ("x+", "x-", "y+", "y-", "zp", "zn", "d")
 RATE = {"d": 400e3}
-COST = {"norm": 1.2, "proj": 0.65, "attn": 0.35, "out": 0.4, "bias": 1.6, "rs": 0.2, "fin": 0.3,
+COST = {"norm": 0.45, "proj": 0.65, "attn": 0.35, "out": 0.4, "bias": 0.5, "rs": 0.2, "fin": 0.3,
         "prep": 1.0, "small": 0.4}
-AHEAD = 3.0
-
-
-H_HOPS = {(0, 0): 4, (1, 0): 3, (0, 1): 4, (1, 1): 3}
+AHEAD = 2.5
+
+
+H_HOPS = {(0, 0): 3, (1, 0): 4, (0, 1): 3, (1, 1): 4}
 R_HOPS = {(0, 0): 4, (1, 0): 3, (0, 1): 4, (1, 1): 3}
 
 
@@ -54,8 +54,7 @@
 
 OUT_NEED = {("p", 0): ("own",), ("p", 1): ("p",), ("p", 2): ("p",), ("p", 3): ("far",),
             ("n", 0): ("n",), ("n", 1): ("n",), ("n", 2): ("far",), ("n", 3): ("far",)}
-RANK = {"zx": (-14.4, 33.6, 2.8, 33.7), "h": (18.2, 34.9), "w": (4.1, 4.4, -0.5, 13.9), "f": -6.4, "s0": -19.3, "s1": 0.0,
-        "s3": 9.7, "f2": -21.4, "s2": -5.3, "r": 58.5}
+RANK = {'zx': (-42.1, 18.4, 22.7, 26.7), 'h': (31.9, 45.6), 'w': (-50.6, 24.8, 11.1, 30.3), 'f': -2.0, 's0': -21.4, 's1': 7.3, 's3': 14.1, 'f2': -69.7, 's2': -40.6, 'r': -5.8}
 
 
 def make_tasks():
@@ -109,17 +108,20 @@
     def theirs(m):
         return [("D", c, m, o) for c in range(2) for o in range(4)]
 
-    add(("bias",), None, 0, [("small",)], 60)
+    for i in range(4):
+        add(("bias", i), None, 0, [("small",)], 60)
     for j in range(2):
-        add(("norm", j), None, 0,
-            [("HD", j)] + [t for t in tasks if t[0] == "H" and t[4] == j], 40 + j)
+        pieces = [("HD", j)] + [t for t in tasks if t[0] == "H" and t[4] == j]
+        for i in range(4):
+            add(("norm", j, i), None, 0, pieces, 40 + j)
+        normed = [("norm", j, i) for i in range(4)] + [("small",)]
         for m in range(3):
-            add(("proj", m, 0, j), None, 0, [("norm", j), ("small",)] + mine(m), 42 + 20 * j + 2 * m)
-            add(("proj", m, 1, j), None, 0, [("norm", j)] + theirs(m), 43 + 20 * j + 2 * m)
+            add(("proj", m, 0, j), None, 0, normed + mine(m), 42 + 20 * j + 2 * m)
+            add(("proj", m, 1, j), None, 0, normed + theirs(m), 43 + 20 * j + 2 * m)
         for cc in range(2):
             for q in range(2):
                 add(("attn", q, cc, j), None, 0,
-                    [("bias",)] + [("proj", m, cc, j) for m in range(3)], 48 + 20 * j)
+                    [("bias", i) for i in range(4)] + [("proj", m, cc, j) for m in range(3)], 48 + 20 * j)
         for n, step in enumerate(("far", "n", "p", "own")):
             add(("out", step, j), None, 0,
                 [("attn", q, cc, j) for q in range(2) for cc in range(2)] + mine(3) + theirs(3),
@@ -181,7 +183,7 @@
         now += COST.get(kind, 0.06)
         finished[tid] = now
         if link:
-            rate = RATE.get(link, 44.0e3) / 1.024e3
+            rate = RATE.get(link, 46.0e3) / 1.024e3
             t = max([now] + [free[one] for one in links]) + kib / rate
             for one in links:
                 free[one] = t
@@ -362,9 +364,9 @@
         elif kind == "small":
             small()
         elif kind == "bias":
-            bias()
+            bias(t[1])
         elif kind == "norm":
-            norm(t[1])
+            norm(t[1], t[2])
         elif kind == "proj":
             _, m, cc, j = t
             who = c if cc == 0 else oc
@@ -435,9 +437,11 @@
         send(pbs.at[c], pbs.at[c], sm.at[0], "d")
         send(mks.at[zl], mks.at[zl], sm.at[1], "zp")
 
-    def bias():
-        recv(pbs.at[oc], sm.at[0])
-        recv(mks.at[oz], sm.at[1])
+    def bias(part):
+        if part == 0:
+            recv(mks.at[oz], sm.at[1])
+        if part == 2:
+            recv(pbs.at[oc], sm.at[0])
         row = lax.broadcasted_iota(jnp.int32, (LEN, LEN), 0)
         lane = lax.broadcasted_iota(jnp.int32, (LEN, LEN), 1)
         rel = lane - row
@@ -447,16 +451,16 @@
             bucket = bucket + jnp.where(dist >= t, 1, 0)
 
         def bias_head(i, _):
-            cc, h = i // 4, i % 4
+            cc, h = c if part < 2 else oc, i % 4
             tab = jnp.zeros((LEN, LEN), F32)
             for b in range(BUCKETS):
                 tab = jnp.where(bucket == b, pbs[cc, b, pl.ds(zl * 4 + h, 1), :], tab)
             bt[cc, pl.ds(pl.multiple_of(h * LEN, LEN), LEN), :] = tab
             return 0
 
-        lax.fori_loop(0, 8, bias_head, 0)
-
-    def norm(j):
+        lax.fori_loop(part * 2, part * 2 + 2, bias_head, 0)
+
+    def norm(j, part):
         def norm_rows(i, _):
             at = pl.ds(pl.multiple_of(i * 16, 16), 16)
             total = jnp.zeros((16, 512), F32)
@@ -471,7 +475,7 @@
                     v * scale * g_ref[:, fb * 512:(fb + 1) * 512]).astype(BF16)
             return 0
 
-        lax.fori_loop(j * 16, j * 16 + 16, norm_rows, 0)
+        lax.fori_loop(j * 16 + part * 4, j * 16 + part * 4 + 4, norm_rows, 0)
 
     def attend(q, cc, j):
         head = lax.broadcasted_iota(jnp.int32, (LEN, 256), 1) // DH

time: 112 us -> 109 us (0.973)
  Pallas kernels: 110 us -> 107 us
    pallas_call x1, Pallas kernels: 110 us -> 107 us  [local(): pl.pallas_call(kernel, out_shape=jax.ShapeDtypeStruct((512, 512), BF16),...]
where the time goes in v4:
time: 109 us
  Pallas kernels  107 us (98%)
  local copies, waits for them, and re-layouts  1.87 us (2%)
    pallas_call x1, Pallas kernels, local(): pl.pallas_call(kernel, out_shape=jax.ShapeDtypeStruct((512, 512), BF16),...  107 us

profile of v4, /device:TPU:1, one launch (start us, length us, event | category | flops | bytes accessed | tf_op | source)
XLA Modules:
  0.0 108.9 jit_solution(6940090264388885780)
XLA Ops:
  0.0 107.0 %t5_attention.1 = bf16[512,512]{1,0:T(8,128)(2,1)} custom-call(bf16[512,512]{1,0:T(8,128)(2,1)} %x_ref.1, f32[1,4096]{1,0:T(1,128)} %g_hbm.1, bf16[128,512]{1,0:T(8,128)(2,1)} %bitcast.7, bf16[128,2,512]{2,1,0:T(2,128)(2,1)} %bitcast.6, bf16[128,512]{1,0:T(8,128)(2,1)} %bitcast.8, f32[8,32]{1,0:T(8,128)} %bitcast.9, s32[4]{0:T(128)} %len_hbm.1), custom_call_target="tpu_custom_call" | custom-call | tf_op jit(solution)/shard_map/t5_attention/pallas_call | solution.py:523
  107.0 1.9 %copy.9 = bf16[512,512]{1,0:T(8,128)(2,1)} copy(bf16[512,512]{1,0:T(8,128)(2,1)} %t5_attention.1) | data formatting | bytes 1048576

commit v5 on v4

--- a/solution.py
+++ b/solution.py
@@ -33,14 +33,15 @@
 
 
 LINKS = ("x+", "x-", "y+", "y-", "zp", "zn", "d")
-RATE = {"d": 400e3}
-COST = {"norm": 0.45, "proj": 0.65, "attn": 0.35, "out": 0.4, "bias": 0.5, "rs": 0.2, "fin": 0.3,
+RATE = {"d": 500e3}
+COST = {"norm": 0.45, "proj": 0.65, "soft": 0.28, "attn": 0.12, "out": 0.4, "bias": 0.5, "rs": 0.2, "fin": 0.3,
         "prep": 1.0, "small": 0.4}
-AHEAD = 2.5
+AHEAD = 2.7
+HOLD = 0.1
 
 
 H_HOPS = {(0, 0): 3, (1, 0): 4, (0, 1): 3, (1, 1): 4}
-R_HOPS = {(0, 0): 4, (1, 0): 3, (0, 1): 4, (1, 1): 3}
+R_HOPS = {(0, 0): 4, (1, 0): 3, (0, 1): 3, (1, 1): 4}
 
 
 def flip(d):
@@ -54,7 +55,7 @@
 
 OUT_NEED = {("p", 0): ("own",), ("p", 1): ("p",), ("p", 2): ("p",), ("p", 3): ("far",),
             ("n", 0): ("n",), ("n", 1): ("n",), ("n", 2): ("far",), ("n", 3): ("far",)}
-RANK = {'zx': (-42.1, 18.4, 22.7, 26.7), 'h': (31.9, 45.6), 'w': (-50.6, 24.8, 11.1, 30.3), 'f': -2.0, 's0': -21.4, 's1': 7.3, 's3': 14.1, 'f2': -69.7, 's2': -40.6, 'r': -5.8}
+RANK = {'zx': (-62.8, -38.1, 16.7, -3.3), 'h': (22.2, 71.8), 'w': (1.9, 27.0, 3.6, 30.5), 'f': -8.7, 's0': -46.4, 's1': 5.5, 's3': 28.7, 'f2': -21.6, 's2': -36.9, 'r': -21.5}
 
 
 def make_tasks():
@@ -95,9 +96,13 @@
             for o in range(4):
                 d = "+-"[(m + cls + o) % 2]
                 add(("S2", cls, m, o), sa + d, 64, [("S", cls, m, o, d)], late + RANK["s2"])
-                add(("D", cls, m, o), "d", 256,
-                    [("S", cls, m, o, "+"), ("S", cls, m, o, "-"), ("S2", cls, m, o)]
-                    + ([("small",)] if o == 0 else []), late)
+                if o < 3:
+                    add(("D", cls, m, o), "d", 256,
+                        [("S", cls, m, o, "+"), ("S", cls, m, o, "-"), ("S2", cls, m, o)]
+                        + ([("small",)] if o == 0 else []), late)
+                    continue
+                for i, need in enumerate((("F2", cls, m), ("S", cls, m, o, "+"), ("S", cls, m, o, "-"), ("S2", cls, m, o))):
+                    add(("D", cls, m, o + i), "d", 64, [need], late)
 
     def mine(m):
         return ([("ZX", m)] + [("F", c, m, d) for c in range(2) for d in "+-"]
@@ -106,7 +111,7 @@
                 + [("S2", c, m, o) for c in range(2) for o in range(4)])
 
     def theirs(m):
-        return [("D", c, m, o) for c in range(2) for o in range(4)]
+        return [("D", c, m, o) for c in range(2) for o in range(7)]
 
     for i in range(4):
         add(("bias", i), None, 0, [("small",)], 60)
@@ -120,8 +125,9 @@
             add(("proj", m, 1, j), None, 0, normed + theirs(m), 43 + 20 * j + 2 * m)
         for cc in range(2):
             for q in range(2):
-                add(("attn", q, cc, j), None, 0,
-                    [("bias", i) for i in range(4)] + [("proj", m, cc, j) for m in range(3)], 48 + 20 * j)
+                add(("soft", q, cc, j), None, 0,
+                    [("bias", i) for i in range(4)] + [("proj", m, cc, j) for m in range(2)], 48 + 20 * j)
+                add(("attn", q, cc, j), None, 0, [("soft", q, cc, j), ("proj", 2, cc, j)], 48 + 20 * j)
         for n, step in enumerate(("far", "n", "p", "own")):
             add(("out", step, j), None, 0,
                 [("attn", q, cc, j) for q in range(2) for cc in range(2)] + mine(3) + theirs(3),
@@ -147,7 +153,7 @@
     free = dict.fromkeys(LINKS, 0.0)
     arrive, finished, order = {}, {}, []
     left = dict(tasks)
-    now = 0.0
+    now, summing = 0.0, False
 
     def ready_at(tid):
         t = 0.0
@@ -159,7 +165,7 @@
         return t
 
     while left:
-        best, soonest = None, None
+        best, soonest, due = None, None, None
         for tid in left:
             link, kib, _, rank = tasks[tid]
             at = ready_at(tid)
@@ -172,12 +178,18 @@
                 key = (0 if link else 1, rank, str(tid))
                 if best is None or key < best[0]:
                     best = (key, tid, links)
-            elif soonest is None or at < soonest:
-                soonest = at
+            else:
+                soonest = at if soonest is None else min(at, soonest)
+                if link:
+                    due = at if due is None else min(at, due)
         if best is None:
             now = soonest
             continue
         _, tid, links = best
+        if summing and not links and due is not None and due < now + COST.get(tid[0], 0.06) - HOLD:
+            now = due
+            continue
+        summing = summing or tid[0] == "R"
         link, kib, _, _ = tasks[tid]
         kind = {"R": "rs"}.get(tid[0], tid[0])
         now += COST.get(kind, 0.06)
@@ -194,7 +206,7 @@
 
 
 def kernel(x_ref, g_hbm, q_hbm, kv_hbm, ow_hbm, pb_hbm, len_hbm, o_ref,
-           wb, hb, nb, qkv, att, ob, sb, rb, bt, pbs, mks, fs, fr,
+           wb, hb, nb, qkv, att, ob, sb, rb, bt, pbs, mks, fs, fr, wts,
            wq, wo, wkv, kvs, g_ref, pbv, lens,
            loc_sem, send_sem, hr, hd, wzs, wf, wf2, ws, ws2, wd, rr, sm, fin):
     dp = lax.axis_index("dp")
@@ -221,7 +233,7 @@
         "zp": dev(zstep("p", 1), xi, yi, c), "zn": dev(zstep("n", 1), xi, yi, c),
         "d": dev(z, xi, yi, oc),
     }
-    pending = []
+    pending, outs = [], []
 
     def send(src, dst, sem, link):
         d = pltpu.make_async_remote_copy(
@@ -283,7 +295,13 @@
         f = axes(cls)[2]
         return (f + (0, 3, 1, 2)[o]) % 4
 
-    def dslice(m, cls, ff, cc):
+    def dslice(m, cls, o, cc):
+        f, s = axes(cls)[2:]
+        ff = fblock(cls, min(o, 3))
+        if o >= 3:
+            s = (s + (0, 3, 1, 2)[o - 3]) % 4
+            bx, by = (ff, s) if cls == 0 else (s, ff)
+            return wb.at[m, cc, zl if cls == 0 else oz, bx, by]
         if cls == 0:
             return wb.at[m, cc, zl, ff]
         return wb.at[m, cc, oz, :, ff]
@@ -340,7 +358,7 @@
             send(b, b, ws2.at[cls, m, o], sa + d)
         elif kind == "D":
             _, cls, m, o = t
-            p = dslice(m, cls, fblock(cls, o), c)
+            p = dslice(m, cls, o, c)
             send(p, p, wd.at[cls, m, o], "d")
         elif kind == "R":
             _, d, r, hh, j = t
@@ -356,9 +374,10 @@
                      + rb[0, 0, hh, j].astype(F32) + rb[1, 0, hh, j].astype(F32)).astype(BF16)
             if hh:
                 fs[j] = value
-                send(fs.at[j], fr.at[j], fin.at[j], "d")
+                send(fs.at[j], o_ref.at[pl.ds((c * 2 + j) * LEN, LEN)], fin.at[j], "d")
             else:
-                o_ref[pl.ds((c * 2 + j) * LEN, LEN), :] = value
+                fr[j] = value
+                outs.append(local(12 + j, fr.at[j], o_ref.at[pl.ds((c * 2 + j) * LEN, LEN)]))
         elif kind == "prep":
             prep()
         elif kind == "small":
@@ -374,6 +393,8 @@
             half = slice(j * 256, j * 256 + 256)
             qkv[m, who, half, :] = jnp.dot(
                 nb[half, :], w, preferred_element_type=F32).astype(BF16)
+        elif kind == "soft":
+            soften(*t[1:])
         elif kind == "attn":
             attend(*t[1:])
         elif kind == "out":
@@ -415,7 +436,7 @@
             recv(blk(m, cls, fblock(cls, o), (s + 2) % 4), ws2.at[cls, m, o])
         elif kind == "D":
             _, cls, m, o = t
-            recv(dslice(m, cls, fblock(cls, o), oc), wd.at[cls, m, o])
+            recv(dslice(m, cls, o, oc), wd.at[cls, m, o])
         elif kind == "R":
             _, d, r, hh, j = t
             recv(rb.at[side(d), r, hh, j], rr.at[side(d), r, hh, j])
@@ -477,11 +498,14 @@
 
         lax.fori_loop(j * 16 + part * 4, j * 16 + part * 4 + 4, norm_rows, 0)
 
-    def attend(q, cc, j):
-        head = lax.broadcasted_iota(jnp.int32, (LEN, 256), 1) // DH
+    def headmask():
+        return lax.broadcasted_iota(jnp.int32, (LEN, 256), 1) // DH
+
+    def soften(q, cc, j):
+        head = headmask()
         who = c if cc == 0 else oc
         at = slice((j * 2 + q) * LEN, (j * 2 + q + 1) * LEN)
-        qq, kk, v = qkv[0, who, at, :], qkv[1, who, at, :], qkv[2, who, at, :]
+        qq, kk = qkv[0, who, at, :], qkv[1, who, at, :]
         zero = jnp.zeros((), BF16)
         qm = jnp.concatenate([jnp.where(head == h, qq, zero) for h in range(4)], axis=0)
         s = lax.dot_general(qm, kk, NT, preferred_element_type=F32) + bt[who]
@@ -489,8 +513,13 @@
         s = jnp.where(seen > 0.5, s, -1e30)
         top = jnp.max(s, axis=-1, keepdims=True)
         e = jnp.exp(s - top)
-        w = (e / jnp.sum(e, axis=-1, keepdims=True)).astype(BF16)
-        mix = jnp.dot(w, v, preferred_element_type=F32)
+        wts[j, q, cc] = (e / jnp.sum(e, axis=-1, keepdims=True)).astype(BF16)
+
+    def attend(q, cc, j):
+        head = headmask()
+        who = c if cc == 0 else oc
+        at = slice((j * 2 + q) * LEN, (j * 2 + q + 1) * LEN)
+        mix = jnp.dot(wts[j, q, cc], qkv[2, who, at, :], preferred_element_type=F32)
         out = jnp.zeros((LEN, 256), F32)
         for h in range(4):
             out = jnp.where(head == h, mix[h * LEN:(h + 1) * LEN], out)
@@ -509,22 +538,22 @@
         if tasks[t][0] and t[0] != "fin" and t not in landed:
             land(t)
     for j in range(2):
-        recv(fr.at[j], fin.at[j])
-        o_ref[pl.ds((oc * 2 + j) * LEN, LEN), :] = fr[j]
+        recv(o_ref.at[pl.ds((oc * 2 + j) * LEN, LEN)], fin.at[j])
+    for d in outs:
+        d.wait()
     for d in pending:
         d.wait_send()
 
 
 def local(hidden_states, norm_gain, query_weight, keyvalue_weight, output_weight,
           position_bias, lengths):
-    vm = pl.BlockSpec(memory_space=pltpu.VMEM)
     hbm = pl.BlockSpec(memory_space=pl.ANY)
     dma = pltpu.SemaphoreType.DMA
     return pl.pallas_call(
         kernel,
         out_shape=jax.ShapeDtypeStruct((512, 512), BF16),
         in_specs=[hbm] * 7,
-        out_specs=vm,
+        out_specs=hbm,
         scratch_shapes=[
             pltpu.VMEM((4, 2, 2, 4, 4, 128, 256), BF16),
             pltpu.VMEM((8, 512, 512), BF16),
@@ -539,6 +568,7 @@
             pltpu.VMEM((2, 8, LEN), F32),
             pltpu.VMEM((2, 128, 512), BF16),
             pltpu.VMEM((2, 128, 512), BF16),
+            pltpu.VMEM((2, 2, 2, 512, 128), BF16),
             pltpu.VMEM((128, 512), BF16),
             pltpu.VMEM((128, 512), BF16),
             pltpu.VMEM((128, 2, 512), BF16),
@@ -546,7 +576,7 @@
             pltpu.VMEM((1, 4096), F32),
             pltpu.VMEM((8, BUCKETS), F32),
             pltpu.SMEM((4,), jnp.int32),
-            dma((12,)),
+            dma((14,)),
             dma((1,)),
             dma((2, 4, 2, 2)),
             dma((2,)),
@@ -555,7 +585,7 @@
             dma((2, 4)),
             dma((2, 4, 4, 2)),
             dma((2, 4, 4)),
-            dma((2, 4, 4)),
+            dma((2, 4, 7)),
             dma((2, 4, 2, 2)),
             dma((2,)),
             dma((2,)),

time: 109 us -> 107 us (0.982)
  Pallas kernels: 107 us -> 105 us
    pallas_call x1, Pallas kernels: 107 us -> 105 us  [local(): pl.pallas_call(kernel, out_shape=jax.ShapeDtypeStruct((512, 512), BF16),...]
where the time goes in v5:
time: 107 us
  Pallas kernels  105 us (98%)
  local copies, waits for them, and re-layouts  1.87 us (2%)
    pallas_call x1, Pallas kernels, local(): pl.pallas_call(kernel, out_shape=jax.ShapeDtypeStruct((512, 512), BF16),...  105 us

profile of v5, /device:TPU:1, one launch (start us, length us, event | category | flops | bytes accessed | tf_op | source)
XLA Modules:
  0.0 106.7 jit_solution(4925859870997982772)
XLA Ops:
  0.0 104.8 %t5_attention.1 = bf16[512,512]{1,0:T(8,128)(2,1)} custom-call(bf16[512,512]{1,0:T(8,128)(2,1)} %x_ref.1, f32[1,4096]{1,0:T(1,128)} %g_hbm.1, bf16[128,512]{1,0:T(8,128)(2,1)} %bitcast.7, bf16[128,2,512]{2,1,0:T(2,128)(2,1)} %bitcast.6, bf16[128,512]{1,0:T(8,128)(2,1)} %bitcast.8, f32[8,32]{1,0:T(8,128)} %bitcast.9, s32[4]{0:T(128)} %len_hbm.1), custom_call_target="tpu_custom_call" | custom-call | tf_op jit(solution)/shard_map/t5_attention/pallas_call | solution.py:552
  104.8 1.9 %copy.9 = bf16[512,512]{1,0:T(8,128)(2,1)} copy(bf16[512,512]{1,0:T(8,128)(2,1)} %t5_attention.1) | data formatting | bytes 1048576

commit v6 on v5

--- a/solution.py
+++ b/solution.py
@@ -34,7 +34,7 @@
 
 LINKS = ("x+", "x-", "y+", "y-", "zp", "zn", "d")
 RATE = {"d": 500e3}
-COST = {"norm": 0.45, "proj": 0.65, "soft": 0.28, "attn": 0.12, "out": 0.4, "bias": 0.5, "rs": 0.2, "fin": 0.3,
+COST = {"norm": 0.45, "proj": 0.35, "soft": 0.28, "attn": 0.12, "out": 0.4, "bias": 0.5, "rs": 0.2, "fin": 0.3,
         "prep": 1.0, "small": 0.4}
 AHEAD = 2.7
 HOLD = 0.1
@@ -121,13 +121,18 @@
             add(("norm", j, i), None, 0, pieces, 40 + j)
         normed = [("norm", j, i) for i in range(4)] + [("small",)]
         for m in range(3):
-            add(("proj", m, 0, j), None, 0, normed + mine(m), 42 + 20 * j + 2 * m)
-            add(("proj", m, 1, j), None, 0, normed + theirs(m), 43 + 20 * j + 2 * m)
+            for cc in range(2):
+                pieces = theirs(m) if cc else mine(m)
+                for part in range(2):
+                    need = [t for t in pieces if (1 if t[0] == "ZX" else t[1]) == part]
+                    if part:
+                        need.append(("proj", m, cc, j, 0))
+                    add(("proj", m, cc, j, part), None, 0, normed + need, 42 + cc + 20 * j + 2 * m)
         for cc in range(2):
             for q in range(2):
                 add(("soft", q, cc, j), None, 0,
-                    [("bias", i) for i in range(4)] + [("proj", m, cc, j) for m in range(2)], 48 + 20 * j)
-                add(("attn", q, cc, j), None, 0, [("soft", q, cc, j), ("proj", 2, cc, j)], 48 + 20 * j)
+                    [("bias", i) for i in range(4)] + [("proj", m, cc, j, 1) for m in range(2)], 48 + 20 * j)
+                add(("attn", q, cc, j), None, 0, [("soft", q, cc, j), ("proj", 2, cc, j, 1)], 48 + 20 * j)
         for n, step in enumerate(("far", "n", "p", "own")):
             add(("out", step, j), None, 0,
                 [("attn", q, cc, j) for q in range(2) for cc in range(2)] + mine(3) + theirs(3),
@@ -206,7 +211,7 @@
 
 
 def kernel(x_ref, g_hbm, q_hbm, kv_hbm, ow_hbm, pb_hbm, len_hbm, o_ref,
-           wb, hb, nb, qkv, att, ob, sb, rb, bt, pbs, mks, fs, fr, wts,
+           wb, hb, nb, qkv, att, ob, sb, rb, bt, pbs, mks, fs, fr, wts, acc,
            wq, wo, wkv, kvs, g_ref, pbv, lens,
            loc_sem, send_sem, hr, hd, wzs, wf, wf2, ws, ws2, wd, rr, sm, fin):
     dp = lax.axis_index("dp")
@@ -387,12 +392,16 @@
         elif kind == "norm":
             norm(t[1], t[2])
         elif kind == "proj":
-            _, m, cc, j = t
+            _, m, cc, j, part = t
             who = c if cc == 0 else oc
-            w = wb[m, who].reshape(4096, 256)
+            zz = oz if part else zl
             half = slice(j * 256, j * 256 + 256)
-            qkv[m, who, half, :] = jnp.dot(
-                nb[half, :], w, preferred_element_type=F32).astype(BF16)
+            depth = pl.ds(pl.multiple_of(zz * 2048, 2048), 2048)
+            value = jnp.dot(nb[half, depth], wb[m, who, zz].reshape(2048, 256), preferred_element_type=F32)
+            if part:
+                qkv[m, who, half, :] = (value + acc[m, cc, j]).astype(BF16)
+            else:
+                acc[m, cc, j] = value
         elif kind == "soft":
             soften(*t[1:])
         elif kind == "attn":
@@ -569,6 +578,7 @@
             pltpu.VMEM((2, 128, 512), BF16),
             pltpu.VMEM((2, 128, 512), BF16),
             pltpu.VMEM((2, 2, 2, 512, 128), BF16),
+            pltpu.VMEM((3, 2, 2, 256, 256), F32),
             pltpu.VMEM((128, 512), BF16),
             pltpu.VMEM((128, 512), BF16),
             pltpu.VMEM((128, 2, 512), BF16),

time: 107 us -> 106 us (level)
  no operation moved by 1% of the time
where the time goes in v6:
time: 106 us
  Pallas kernels  104 us (98%)
  local copies, waits for them, and re-layouts  1.87 us (2%)
    pallas_call x1, Pallas kernels, local(): pl.pallas_call(kernel, out_shape=jax.ShapeDtypeStruct((512, 512), BF16),...  104 us

profile of v6, /device:TPU:1, one launch (start us, length us, event | category | flops | bytes accessed | tf_op | source)
XLA Modules:
  0.0 105.9 jit_solution(4979773872502543869)
XLA Ops:
  0.0 104.0 %t5_attention.1 = bf16[512,512]{1,0:T(8,128)(2,1)} custom-call(bf16[512,512]{1,0:T(8,128)(2,1)} %x_ref.1, f32[1,4096]{1,0:T(1,128)} %g_hbm.1, bf16[128,512]{1,0:T(8,128)(2,1)} %bitcast.7, bf16[128,2,512]{2,1,0:T(2,128)(2,1)} %bitcast.6, bf16[128,512]{1,0:T(8,128)(2,1)} %bitcast.8, f32[8,32]{1,0:T(8,128)} %bitcast.9, s32[4]{0:T(128)} %len_hbm.1), custom_call_target="tpu_custom_call" | custom-call | tf_op jit(solution)/shard_map/t5_attention/pallas_call | solution.py:561
  104.0 1.9 %copy.9 = bf16[512,512]{1,0:T(8,128)(2,1)} copy(bf16[512,512]{1,0:T(8,128)(2,1)} %t5_attention.1) | data formatting | bytes 1048576
